TPU v7x, 256 devices: a whole 4x4x8 slice. The times are simulated.
256 devices in a mesh: expert: 32 (over x, y, core), dp: 8 (over z).
Axes of the slice: x: 4, y: 4, z: 8, core: 2. Of those that a mesh axis runs over, the one named last changes fastest.
Arguments:
- patches: bfloat16 [65536, 1024], P(('expert', 'dp')), may hold values from -6 to 6
- router_weight: bfloat16 [1024, 32], replicated, may hold values from -0.1875 to 0.1875
- router_bias: float32 [32], replicated, may hold values from -1.5 to 1.5
- noise: float32 [65536, 32], P(('expert', 'dp')), may hold values from -5 to 5
- top_experts: int32 [65536, 2], P(('expert', 'dp')), may hold values from 0 to 31, all different within a row; in each aligned block of 256 rows (0 to 255, 256 to 511, ...) at most 20 rows name the same one
- threshold_expert: int32 [65536], P(('expert', 'dp')), may hold values from 0 to 31
- w_in: bfloat16 [32, 1024, 2048], P('expert'), may hold values from -0.1875 to 0.1875
- w_out: bfloat16 [32, 2048, 1024], P('expert'), may hold values from -0.125 to 0.125
- out_grad: bfloat16 [65536, 1024], P(('expert', 'dp')), may hold values from -24 to 24
Outputs:
- patch_grad: bfloat16 [65536, 1024], P(('expert', 'dp'))
- w_in_grad: bfloat16 [32, 1024, 2048], P('expert', None, 'dp')
- w_out_grad: bfloat16 [32, 2048, 1024], P('expert', 'dp')
- router_weight_grad: float32 [1024, 32], replicated
- router_bias_grad: float32 [32], replicated
Inputs may be any that keep to these rules, and one draw needn't show every extreme that they name: `top_experts`: the two experts of a patch differ; among the patches of one device no expert is named more than 20 times.
All inputs are finite; a program needn't handle non-finite values.
Results may differ from a plain program's by a relative error of at most 0.0062.
The roundings to bfloat16 on the way count: a program that leaves them out, or rounds other values in their place, can miss the bound.
Values may be sent and summed in bfloat16 or wider, within the bound.
A program may use at most 128 MiB of HBM per device.

v0:
```python
import jax
import jax.numpy as jnp
from jax import lax
from jax.sharding import Mesh
from jax.sharding import PartitionSpec as P

EXPERT = ("expert_0", "expert_1", "expert_2")
EXPERT_DP = ("expert_0", "expert_1", "expert_2", "dp")


noise_std = 1.0
aux_weight = 1.0
inv_root_two = 0.7071067811865476
inv_root_tau = 0.3989422804014327


def over_axes(shard, axes):
    for axis in axes:
        shard = lax.psum(shard, axis)
    return shard


def sent_together(arrays, axis, split_dim, concat_dim, along):
    columns = [a.reshape(*a.shape[:along], -1) for a in arrays]
    both = jnp.concatenate(columns, axis=along)
    filled, at, gathered = (
        lax.all_to_all(both, axis, split_axis=split_dim, concat_axis=concat_dim, tiled=True),
        0,
        [],
    )
    for a, column in zip(arrays, columns):
        share = filled[..., at : at + column.shape[along]]
        gathered.append(share.reshape(*share.shape[:along], *a.shape[along:]))
        at += column.shape[along]
    return tuple(gathered)


def gelu_tanh(values):
    return jax.nn.gelu(values, approximate=True)


def spread_grad(values):
    number = values.shape[0]
    average = jnp.mean(values)
    spread = jnp.mean((values - average) ** 2)
    return (2.0 * (values - average) - 2.0 * spread / average) / (number * average * average)


def expert_local(rows_in, rows_grad, rows_gate, w_first, w_second):
    hidden = jnp.dot(rows_in, w_first, preferred_element_type=jnp.float32)
    active, pullback = jax.vjp(gelu_tanh, hidden)
    active_low = lax.optimization_barrier(active.astype(jnp.bfloat16))
    back_proj = jnp.dot(rows_grad, w_second.T, preferred_element_type=jnp.float32)
    gate_col = rows_gate.astype(jnp.float32)[:, None]
    gate_terms = jnp.sum(back_proj * active_low.astype(jnp.float32), axis=-1)
    hidden_grad = pullback(gate_col * back_proj)[0].astype(jnp.bfloat16)
    scaled_grad = (gate_col * rows_grad.astype(jnp.float32)).astype(jnp.bfloat16)
    first_grad = jnp.dot(rows_in.T, hidden_grad, preferred_element_type=jnp.float32)
    second_grad = jnp.dot(active_low.T, scaled_grad, preferred_element_type=jnp.float32)
    return (first_grad, second_grad, hidden_grad, gate_terms)


def expert_terms(rows_in, rows_grad, rows_gate, w_first, w_second):
    first_grad, second_grad, hidden_grad, gate_terms = expert_local(
        rows_in, rows_grad, rows_gate, w_first, w_second
    )
    rows_back = jnp.dot(hidden_grad, w_first.T, preferred_element_type=jnp.float32)
    return (first_grad, second_grad, rows_back, gate_terms)


def on_device(
    patches, router_weight, router_bias, noise, top_experts, threshold_expert, w_in, w_out, out_grad
):
    tok_rows = patches.shape[0]
    width = patches.shape[1]
    experts = router_weight.shape[1]
    capacity = 5 * tok_rows // (2 * experts)
    slots = experts * capacity
    total_tokens = tok_rows * lax.axis_size(EXPERT) * lax.axis_size("dp")
    logits = jnp.dot(patches, router_weight, preferred_element_type=jnp.float32) + router_bias
    noisy = logits + noise_std * noise
    probs = jax.nn.softmax(noisy, axis=-1)
    expert_ids = lax.broadcasted_iota(jnp.int32, (1, experts), 1)
    thresh_hot = threshold_expert[:, None] == expert_ids
    base = jnp.sum(jnp.where(thresh_hot, noisy, 0.0), axis=-1, keepdims=True)
    zscore = (logits - base) / noise_std
    importance, load = (
        over_axes(jnp.sum(probs, axis=0), EXPERT_DP),
        over_axes(jnp.sum(0.5 * (1.0 + lax.erf(zscore * inv_root_two)), axis=0), EXPERT_DP),
    )
    top_hot = top_experts[:, :, None] == expert_ids[None]
    gates = jnp.sum(jnp.where(top_hot, probs[:, None, :], 0.0), axis=-1).astype(jnp.bfloat16)
    flat = top_experts.reshape(-1)
    flat_hot = (flat[:, None] == expert_ids).astype(jnp.int32)
    before = jnp.sum((jnp.cumsum(flat_hot, axis=0) - flat_hot) * flat_hot, axis=-1)
    slot_ids = flat * capacity + before
    slot_index = lax.broadcasted_iota(jnp.int32, (slots, 1), 0)
    assign = (slot_index == slot_ids[None, :]).astype(jnp.bfloat16)
    assign_tok = jnp.sum(assign.reshape(slots, tok_rows, 2), axis=-1)
    sent_in = (
        jnp.dot(assign_tok, patches, preferred_element_type=jnp.float32)
        .astype(jnp.bfloat16)
        .reshape(experts, capacity, width)
    )
    sent_grad = (
        jnp.dot(assign_tok, out_grad, preferred_element_type=jnp.float32)
        .astype(jnp.bfloat16)
        .reshape(experts, capacity, width)
    )
    sent_gate = (
        jnp.dot(assign, gates.reshape(-1), preferred_element_type=jnp.float32)
        .astype(jnp.bfloat16)
        .reshape(experts, capacity)
    )
    recv_in, recv_grad, recv_gate = (
        lax.all_to_all(sent_in, EXPERT, split_axis=0, concat_axis=0, tiled=True),
        lax.all_to_all(sent_grad, EXPERT, split_axis=0, concat_axis=0, tiled=True),
        lax.all_to_all(sent_gate, EXPERT, split_axis=0, concat_axis=0, tiled=True),
    )
    rows_in = recv_in.reshape(slots, width)
    rows_grad = recv_grad.reshape(slots, width)
    rows_gate = recv_gate.reshape(slots)
    w_first = w_in[0]
    w_second = w_out[0]
    first_grad, second_grad, rows_back, gate_terms = expert_terms(
        rows_in, rows_grad, rows_gate, w_first, w_second
    )
    first_part, second_part = (
        lax.psum_scatter(first_grad, "dp", scatter_dimension=1, tiled=True),
        lax.psum_scatter(second_grad, "dp", scatter_dimension=0, tiled=True),
    )
    back_rows = rows_back.astype(jnp.bfloat16).reshape(experts, capacity, width)
    back_gate = gate_terms.astype(jnp.bfloat16).reshape(experts, capacity)
    home_rows, home_gate = sent_together((back_rows, back_gate), EXPERT, 0, 0, 2)
    expert_back = jnp.dot(
        assign_tok.T, home_rows.reshape(slots, width), preferred_element_type=jnp.float32
    )
    gate_grad = jnp.dot(
        home_gate.reshape(slots), assign, preferred_element_type=jnp.float32
    ).reshape(tok_rows, 2)
    total_weight = aux_weight * total_tokens
    imp_coef = total_weight * spread_grad(importance)
    load_coef = total_weight * spread_grad(load)
    score_grad = jnp.sum(jnp.where(top_hot, gate_grad[:, :, None], 0.0), axis=1) + imp_coef[None, :]
    noisy_grad = probs * (score_grad - jnp.sum(probs * score_grad, axis=-1, keepdims=True))
    z_grad = load_coef[None, :] * inv_root_tau * jnp.exp(-0.5 * zscore * zscore)
    logit_grad = (
        noisy_grad
        + z_grad / noise_std
        - jnp.where(thresh_hot, jnp.sum(z_grad, axis=-1, keepdims=True) / noise_std, 0.0)
    )
    logit_low = logit_grad.astype(jnp.bfloat16)
    router_back = jnp.dot(logit_low, router_weight.T, preferred_element_type=jnp.float32)
    patch_grad = (expert_back + router_back).astype(jnp.bfloat16)
    weight_part = jnp.dot(patches.T, logit_low, preferred_element_type=jnp.float32)
    router_weight_grad, router_bias_grad = lax.psum(
        (weight_part, jnp.sum(logit_grad, axis=0)), EXPERT_DP
    )
    return (
        patch_grad,
        first_part.astype(jnp.bfloat16)[None],
        second_part.astype(jnp.bfloat16)[None],
        router_weight_grad,
        router_bias_grad,
    )


def solution(mesh):
    torus = Mesh(
        mesh.devices.reshape(4, 4, 2, mesh.shape["dp"]), ("expert_0", "expert_1", "expert_2", "dp")
    )
    in_specs = (
        P(EXPERT_DP, None),
        P(),
        P(),
        P(EXPERT_DP, None),
        P(EXPERT_DP, None),
        P(EXPERT_DP),
        P(EXPERT, None, None),
        P(EXPERT, None, None),
        P(EXPERT_DP, None),
    )
    out_specs = (P(EXPERT_DP, None), P(EXPERT, None, "dp"), P(EXPERT, "dp", None), P(), P())
    return jax.shard_map(
        on_device, mesh=torus, in_specs=in_specs, out_specs=out_specs, check_vma=False
    )
```

profile of v0, /device:TPU:1, one launch (start us, length us, event | category | flops | bytes accessed | tf_op | source)
XLA Modules:
  0.0 530.2 jit_solution(71132456940397908)
XLA Ops:
  9.2 1.2 reduce-window.6
  10.6 1.2 fusion.39
  14.8 8.6 %all-to-all-start = ((bf16[32,1,20]{2,1,0:T(2,128)(2,1)}), bf16[32,1,20]{2,1,0:T(2,128)(2,1)S(1)}, u32[]{:S(2)}, u32[]{:S(2)}) async-start(bf16[32,1,20]{2,1,0:T(2,128)(2,1)} %all_to_all.20), calls=%async_computation | async-start | bytes 32768 | tf_op jit(solution)/shard_map/all_to_all | solution.py:118
  25.8 1.3 reshape.135
  27.1 3.2 all-to-all-done
  30.3 4.3 all-to-all-start.2
  34.6 1.7 convolution_convert_fusion.1
  36.3 1.3 reshape.133
  37.6 19.8 %all-to-all-done.2 = bf16[32,20,1024]{2,1,0:T(8,128)(2,1)S(1)} async-done(((bf16[32,20,1024]{2,1,0:T(8,128)(2,1)}), bf16[32,20,1024]{2,1,0:T(8,128)(2,1)S(1)}, u32[]{:S(2)}, u32[]{:S(2)}) %all-to-all-start.2) | async-done | bytes 1310752 | tf_op jit(solution)/shard_map/all_to_all | solution.py:116
  57.3 4.8 all-to-all-start.1
  62.7 8.1 %multiply_convert_fusion = (bf16[640,2048]{1,0:T(8,128)(2,1)}, f32[640,2048]{1,0:T(8,128)}) fusion(bf16[640,1024]{1,0:T(8,128)(2,1)S(1)} %reshape.136, bf16[1,1024,2048]{2,1,0:T(8,128)(2,1)} %param.15), kind=kOutput, calls=%fused_computation.10 | convolution fusion | flops 2696151040 | bytes 13369344 | tf_op jit(solution)/shard_map/dot_general | solution.py:50
  70.8 14.2 %all-to-all-done.1 = bf16[32,20,1024]{2,1,0:T(8,128)(2,1)} async-done(((bf16[32,20,1024]{2,1,0:T(8,128)(2,1)}), bf16[32,20,1024]{2,1,0:T(8,128)(2,1)}, u32[]{:S(2)}, u32[]{:S(2)}) %all-to-all-start.1) | async-done | bytes 1310752 | tf_op jit(solution)/shard_map/all_to_all | solution.py:117
  85.0 2.3 reshape.134
  87.3 9.3 %fusion.6 = (bf16[640,2048]{1,0:T(8,128)(2,1)S(1)}, bf16[640]{0:T(1024)(128)(2,1)S(1)}) fusion(f32[640,2048]{1,0:T(8,128)} %get-tuple-element.25, f32[640]{0:T(1024)S(1)} %reshape.139, bf16[640,2048]{1,0:T(8,128)(2,1)} %get-tuple-element.24, bf16[640,1024]{1,0:T(8,128)(2,1)S(1)} %reshape.134, bf16[1,2048,1024]{2,1,0:T(8,128)(2,1)} %param.16), kind=kOutput, calls=%fused_computation.8 | convolution fusion | flops 2715811328 | bytes 15994624 | tf_op jit(solution)/shard_map/dot_general | solution.py:53
  96.5 1.5 copy-done.6
  98.0 5.7 %fusion.41 = f32[1024,2048]{1,0:T(8,128)} fusion(bf16[640,1024]{1,0:T(8,128)(2,1)S(1)} %reshape.136, bf16[640,2048]{1,0:T(8,128)(2,1)S(1)} %get-tuple-element.21), kind=kOutput, calls=%fused_computation.78 | convolution fusion | flops 2684354560 | bytes 12320768 | tf_op jit(solution)/shard_map/dot_general | solution.py:58
  103.9 7.6 %fusion.17 = f32[2048,1024]{1,0:T(8,128)} fusion(bf16[640,2048]{1,0:T(8,128)(2,1)} %get-tuple-element.24, bf16[640,1024]{1,0:T(8,128)(2,1)S(1)} %reshape.134, f32[640]{0:T(1024)S(1)} %reshape.139), kind=kOutput, calls=%fused_computation.25 | convolution fusion | flops 2686320640 | bytes 12323328 | tf_op jit(solution)/shard_map/dot_general | solution.py:59
  112.5 6.7 %fusion.13 = bf16[640,1024]{1,0:T(8,128)(2,1)S(1)} fusion(bf16[640,2048]{1,0:T(8,128)(2,1)} %copy-done.6, bf16[1,1024,2048]{2,1,0:T(8,128)(2,1)} %param.15), kind=kOutput, calls=%fused_computation.20 | convolution fusion | flops 2685009920 | bytes 8126464 | tf_op jit(solution)/shard_map/dot_general | solution.py:67
  119.5 2.4 pad_maximum_fusion
  121.9 4.3 all-to-all-start.3
  126.2 24.7 %all-reduce.2 = (f32[32]{0:T(128)S(1)}, f32[32]{0:T(128)S(1)}) all-reduce(f32[32]{0:T(128)S(1)} %get-tuple-element.26, f32[32]{0:T(128)S(1)} %get-tuple-element.17), channel_id=1, replica_groups=mesh['expert_0'=4,'expert_1'=4,'expert_2'=2,'dp'=8] {'expert_0'}, use_global_device_ids=true, to_apply=%region_19.20 | all-reduce | flops 64 | bytes 512 | tf_op jit(solution)/shard_map/psum | solution.py:19
  150.9 9.2 %all-reduce.1 = (f32[32]{0:T(128)S(1)}, f32[32]{0:T(128)S(1)}) all-reduce(f32[32]{0:T(128)S(1)} %get-tuple-element.11, f32[32]{0:T(128)S(1)} %get-tuple-element.12), channel_id=1, replica_groups=mesh['expert_0'=4,'expert_1'=4,'expert_2'=2,'dp'=8] {'expert_1'}, use_global_device_ids=true, to_apply=%region_20.21 | all-reduce | flops 64 | bytes 512 | tf_op jit(solution)/shard_map/psum | solution.py:19
  160.2 4.7 all-reduce.3
  164.8 18.0 %all-reduce = (f32[32]{0:T(128)S(1)}, f32[32]{0:T(128)S(1)}) all-reduce(f32[32]{0:T(128)S(1)} %get-tuple-element.13, f32[32]{0:T(128)S(1)} %get-tuple-element.14), channel_id=1, replica_groups=mesh['expert_0'=4,'expert_1'=4,'expert_2'=2,'dp'=8] {'dp'}, use_global_device_ids=true, to_apply=%region_22.23 | all-reduce | flops 64 | bytes 512 | tf_op jit(solution)/shard_map/psum | solution.py:19
  191.6 76.5 %psum.79 = f32[32]{0:T(128)} all-reduce(f32[32]{0:T(128)S(1)} %get-tuple-element.15), channel_id=1, replica_groups=mesh['expert_0'=4,'expert_1'=4,'expert_2'=2,'dp'=8] {'expert_0','expert_..., use_global_device_ids=true, to_apply=%region_30.31 | all-reduce | flops 32 | bytes 256 | tf_op jit(solution)/shard_map/psum | solution.py:156
  268.1 1.4 slice.17
  269.5 2.3 reshape.138
  274.5 2.1 convert_bitcast_fusion.1
  276.6 19.0 %reduce-scatter.5.cloned.1.call-done = f32[256,1024]{1,0:T(8,128)} async-done(((f32[2048,1024]{1,0:T(8,128)}), f32[256,1024]{1,0:T(8,128)}) %reduce-scatter.5.cloned.1.call-update) | async-done | bytes 1048592 | tf_op jit(solution)/shard_map/reduce_scatter | solution.py:130
  295.5 2.1 convert_bitcast_fusion
  297.6 223.6 %all-reduce.6.cloned.1.call-done = f32[1024,32]{0,1:T(8,128)} async-done(((f32[1024,32]{0,1:T(8,128)}), f32[1024,32]{0,1:T(8,128)}) %all-reduce.6.cloned.1.call-update) | async-done | bytes 131088 | tf_op jit(solution)/shard_map/psum | solution.py:156
  521.2 1.6 copy.58
  (67 shorter events, 16.3 us)
Async XLA Ops:
  8.0 2.6 copy-start
  14.8 15.5 %all-to-all-start = ((bf16[32,1,20]{2,1,0:T(2,128)(2,1)}), bf16[32,1,20]{2,1,0:T(2,128)(2,1)S(1)}, u32[]{:S(2)}, u32[]{:S(2)}) async-start(bf16[32,1,20]{2,1,0:T(2,128)(2,1)} %all_to_all.20), calls=%async_computation | async-start | bytes 32768 | tf_op jit(solution)/shard_map/all_to_all | solution.py:118
  24.6 0.7 copy-start.1
  30.3 27.0 %all-to-all-start.2 = ((bf16[32,20,1024]{2,1,0:T(8,128)(2,1)}), bf16[32,20,1024]{2,1,0:T(8,128)(2,1)S(1)}, u32[]{:S(2)}, u32[]{:S(2)}) async-start(bf16[32,20,1024]{2,1,0:T(8,128)(2,1)} %reshape.135), calls=%async_computation.2 | async-start | bytes 3145728 | tf_op jit(solution)/shard_map/all_to_all | solution.py:116
  57.3 27.6 %all-to-all-start.1 = ((bf16[32,20,1024]{2,1,0:T(8,128)(2,1)}), bf16[32,20,1024]{2,1,0:T(8,128)(2,1)}, u32[]{:S(2)}, u32[]{:S(2)}) async-start(bf16[32,20,1024]{2,1,0:T(8,128)(2,1)} %reshape.133), calls=%async_computation.1 | async-start | bytes 3145728 | tf_op jit(solution)/shard_map/all_to_all | solution.py:117
  62.2 212.3 %reduce-scatter.3.cloned.1.call-start = ((), (), s32[]{:S(2)}) async-start(), calls=%async_computation.6 | async-start | bytes 9437184 | tf_op jit(solution)/shard_map/reduce_scatter | solution.py:129
  96.5 1.5 copy-start.6
  103.7 191.8 %reduce-scatter.5.cloned.1.call-start = ((), (), s32[]{:S(2)}) async-start(), calls=%async_computation.7 | async-start | bytes 9437184 | tf_op jit(solution)/shard_map/reduce_scatter | solution.py:130
  121.9 69.4 %copy-start.4 = (s32[256,2]{0,1:T(2,128)S(1)}, s32[256,2]{0,1:T(2,128)}, u32[]{:S(2)}) copy-start(s32[256,2]{0,1:T(2,128)} %param.13) | copy-start | bytes 6148
  121.9 69.5 %copy-start.5 = (s32[256]{0:T(256)S(1)}, s32[256]{0:T(256)}, u32[]{:S(2)}) copy-start(s32[256]{0:T(256)} %param.14) | copy-start | bytes 3076
  121.9 68.1 %all-to-all-start.3 = ((bf16[32,20,1025]{2,1,0:T(8,128)(2,1)}), bf16[32,20,1025]{2,1,0:T(8,128)(2,1)S(1)}, u32[]{:S(2)}, u32[]{:S(2)}) async-start(bf16[32,20,1025]{2,1,0:T(8,128)(2,1)} %pad_maximum_fusion), calls=%async_computation.3 | async-start | bytes 3538944 | tf_op jit(solution)/shard_map/all_to_all | solution.py:27
  126.2 395.1 %all-reduce.6.cloned.1.call-start = ((), (), s32[]{:S(2)}) async-start(), calls=%async_computation.8 | async-start | bytes 262144 | tf_op jit(solution)/shard_map/psum | solution.py:156
  268.1 4.6 copy-start.2
  269.5 3.8 copy-start.3
Sparse Core Ops, SparseCore 0:
  103.8 94.1 reduce-scatter.2
  200.6 94.8 reduce-scatter.4
Sparse Core Ops, SparseCore 1:
  274.5 246.6 all-reduce.5
where the time goes:
time: 532 us; the launch traced here: 530 us
  waiting for transfers between devices  280 us (53%)
  blocking collectives  133 us (25%)
  matrix products  43.4 us (8%)
  starting transfers between devices  22.2 us (4%)
  between operations  19.7 us (4%)
  local copies, waits for them, and re-layouts  17.5 us (3%)
  other arithmetic  14.4 us (3%)
    psum x1, waiting for transfers between devices, on_device(): lax.psum((weight_part, jnp.sum(logit_grad, axis=0)), EXPERT_DP)  224 us
    psum x1, blocking collectives, on_device(): lax.psum((weight_part, jnp.sum(logit_grad, axis=0)), EXPERT_DP)  76.5 us
    psum x4, blocking collectives, over_axes(): shard = lax.psum(shard, axis)  56.6 us
    all_to_all x1, waiting for transfers between devices, on_device(): lax.all_to_all(sent_in, EXPERT, split_axis=0, concat_axis=0, tiled=True)  19.8 us
    reduce_scatter x1, waiting for transfers between devices, on_device(): lax.psum_scatter(second_grad, 'dp', scatter_dimension=0, tiled=True)  19 us
    all_to_all x1, waiting for transfers between devices, on_device(): lax.all_to_all(sent_grad, EXPERT, split_axis=0, concat_axis=0, tiled=True)  14.2 us
  transfers between devices with their start and end apart: 7, of which 5 were waited for; matrix products, arithmetic and copies ran while one was open for 9% of the time, Pallas kernels for 0%

commit v1 on v0

v1 whole, which is shorter than its diff:
```python
import functools
import math

import jax
import jax.numpy as jnp
from jax import lax
from jax.experimental import pallas as pl
from jax.experimental.pallas import tpu as pltpu
from jax.sharding import PartitionSpec as P

F32 = jnp.float32
BF16 = jnp.bfloat16
MESH = pl.DeviceIdType.MESH
MAIN = 16
REST = 4
SPLIT = 4
NSUB = 2
inv_root_two = 0.7071067811865476
inv_root_tau = 0.3989422804014327
gelu_k = math.sqrt(2.0 / math.pi)


def dot(a, b):
    return jnp.dot(a, b, preferred_element_type=F32)


def dot_nt(a, b):
    return lax.dot_general(a, b, (((1,), (1,)), ((), ())), preferred_element_type=F32)


def iota(shape, dim):
    return lax.broadcasted_iota(jnp.int32, shape, dim)


def hot(mask):
    return jnp.where(mask, 1.0, 0.0).astype(BF16)


def wait_bytes(ref, sem):
    pltpu.make_async_copy(ref, ref, sem).wait()


def kernel(
    E, NZ, TOTAL,
    patches, rwT, bias, noiseT, topT, thr, og, w_in_hbm, w_out_hbm,
    pg, wiT, wo, rgT, rb,
    w_in, w_out, w_inT, sel, selr, selT, selrT, send_x, send_g, recv_x, recv_g,
    send_b, recv_b, X, G, SG, AT, HT, rbT, growr, gt, cw0, cw, ccw0, ccw,
    probs_s, z_s, llT_s, stat, sr1, ss2, sr2, ws1, wr1, ws2, wr2, ws3, wr3, wsem, px, ring_sem,
):
    T, D = patches.shape
    F = w_out.shape[0]
    FC = F // NZ
    SUB = FC // NSUB
    QD = D // SPLIT
    S = E * MAIN
    R = E * REST
    ROWS = S + R
    me = lax.axis_index("expert")
    z = lax.axis_index("dp")

    load_in = pltpu.make_async_copy(w_in_hbm, w_in, wsem.at[0])
    load_out = pltpu.make_async_copy(w_out_hbm, w_out, wsem.at[1])
    load_in.start()
    load_out.start()

    barrier = pltpu.get_barrier_semaphore()

    def greet_plane(p, c):
        pl.semaphore_signal(
            barrier, inc=1, device_id=(lax.rem(me + p, E), z), device_id_type=MESH
        )
        return c

    def greet_line(p, c):
        pl.semaphore_signal(
            barrier, inc=1, device_id=(me, lax.rem(z + p, NZ)), device_id_type=MESH
        )
        return c

    lax.fori_loop(1, E, greet_plane, 0)
    lax.fori_loop(1, NZ, greet_line, 0)

    def to_plane(src, by_peer, dst, rows, k):
        def body(i, c):
            half = (i + 1) // 2
            p = half + (1 - lax.rem(i, 2)) * (E - 2 * half)
            peer = lax.rem(me + p, E)
            if by_peer:
                piece = src.at[pl.ds(pl.multiple_of(peer * rows, rows), rows)]
            else:
                piece = src
            pltpu.make_async_remote_copy(
                src_ref=piece,
                dst_ref=dst.at[pl.ds(pl.multiple_of(me * rows, rows), rows)],
                send_sem=px.at[2 * k],
                recv_sem=px.at[2 * k + 1],
                device_id=(peer, z),
                device_id_type=MESH,
            ).start()
            return c

        lax.fori_loop(1, E, body, 0)

    def to_line(src, dst, rows, k):
        def body(p, c):
            pltpu.make_async_remote_copy(
                src_ref=src,
                dst_ref=dst.at[pl.ds(pl.multiple_of(z * rows, rows), rows)],
                send_sem=px.at[2 * k],
                recv_sem=px.at[2 * k + 1],
                device_id=(me, lax.rem(z + p, NZ)),
                device_id_type=MESH,
            ).start()
            return c

        lax.fori_loop(1, NZ, body, 0)

    def own_block(src, by_peer, dst, at, rows):
        here = pl.ds(pl.multiple_of(at * rows, rows), rows)
        dst[here, :] = src[here, :] if by_peer else src[...]

    def received(dst, rows, peers, k):
        wait_bytes(dst.at[pl.ds(0, (peers - 1) * rows)], px.at[2 * k + 1])

    def sent(dst, rows, peers, k):
        wait_bytes(dst.at[pl.ds(0, (peers - 1) * rows)], px.at[2 * k])

    experts = iota((E, T), 0)
    member = (topT[0:1, :] == experts) | (topT[1:2, :] == experts)
    earlier = hot(iota((T, T), 0) < iota((T, T), 1))
    before = dot(hot(member), earlier)
    code = jnp.where(member, before, -1.0).astype(BF16)
    spread = hot(iota((S, E), 0) // MAIN == iota((S, E), 1))
    code_rows = dot(spread, code)
    place = lax.rem(iota((S, T), 0), MAIN)
    sel[...] = hot(code_rows == place.astype(F32))
    is_rest = code_rows == (lax.rem(place, REST) + MAIN).astype(F32)
    for q in range(SPLIT):
        selr[pl.ds(q * S, S), :] = hot(is_rest & (place // REST == q))

    RB = min(S, 128)

    def pack_rows(src, dst):
        def body(i, c):
            rows = pl.ds(pl.multiple_of(i * RB, RB), RB)
            dst[rows, 0:D] = dot(sel[rows, :], src[...]).astype(BF16)
            acc = jnp.zeros((RB, QD), F32)
            for q in range(SPLIT):
                pick = selr[pl.ds(pl.multiple_of(q * S + i * RB, RB), RB), :]
                acc += dot(pick, src[:, q * QD : (q + 1) * QD])
            dst[rows, D : D + QD] = acc.astype(BF16)
            return c

        lax.fori_loop(0, S // RB, body, 0)

    pack_rows(patches, send_x)
    pl.semaphore_wait(barrier, E + NZ - 2)
    to_plane(send_x, True, recv_x, MAIN, 0)
    own_block(send_x, True, recv_x, me, MAIN)

    logits = dot_nt(rwT[...], patches[...]) + bias[...]
    noisy = logits + noiseT[...]
    top = jnp.max(noisy, axis=0, keepdims=True)
    powers = jnp.exp(noisy - top)
    probs = powers / jnp.sum(powers, axis=0, keepdims=True)
    thresh = thr[...] == experts
    base = jnp.sum(jnp.where(thresh, noisy, 0.0), axis=0, keepdims=True)
    zscore = logits - base
    probs_s[...] = probs
    z_s[...] = zscore
    prob_rows = dot(spread, probs.astype(BF16))
    gate_main = jnp.sum(prob_rows * sel[...].astype(F32), axis=1, keepdims=True)
    gate_rest = jnp.sum(jnp.where(is_rest, prob_rows, 0.0), axis=1, keepdims=True)
    low_lanes = iota((S, 128), 1) < 64
    send_g[:, D + QD : D + QD + 128] = jnp.where(low_lanes, gate_main, gate_rest).astype(BF16)
    pack_rows(og, send_g)
    to_plane(send_g, True, recv_g, MAIN, 1)
    own_block(send_g, True, recv_g, me, MAIN)

    importance = jnp.sum(probs, axis=1, keepdims=True)
    load = jnp.sum(0.5 * (1.0 + lax.erf(zscore * inv_root_two)), axis=1, keepdims=True)
    row_id = iota((E, 128), 0)
    lane_id = iota((E, 128), 1)
    both = jnp.where(lane_id == row_id, importance, 0.0) + jnp.where(
        lane_id == row_id + E, load, 0.0
    )
    stat[...] = jnp.broadcast_to(jnp.sum(both, axis=0, keepdims=True), (8, 128))
    to_plane(stat, False, sr1, 8, 2)
    own_block(stat, False, sr1, me, 8)

    eye_t = hot(iota((T, T), 0) == iota((T, T), 1))
    selT[...] = dot_nt(eye_t, sel[...]).astype(BF16)
    for q in range(SPLIT):
        selrT[pl.ds(q * T, T), :] = dot_nt(eye_t, selr[pl.ds(q * S, S), :]).astype(BF16)
    load_in.wait()
    load_out.wait()

    def turn(i, c):
        cols = pl.ds(pl.multiple_of(i * 256, 256), 256)
        w_inT[cols, :] = w_in[:, cols].T
        return c

    lax.fori_loop(0, F // 256, turn, 0)

    def unpack_pick(q):
        r = iota((R, S), 0)
        return hot(iota((R, S), 1) == (r // REST) * MAIN + q * REST + lax.rem(r, REST))

    def pack_pick(q):
        r = iota((S, R), 1)
        return hot(iota((S, R), 0) == (r // REST) * MAIN + q * REST + lax.rem(r, REST))

    def unpack(src, dst):
        dst[0:S, :] = src[:, 0:D]
        for q in range(SPLIT):
            dst[S:ROWS, q * QD : (q + 1) * QD] = dot(
                unpack_pick(q), src[:, D : D + QD]
            ).astype(BF16)

    received(recv_x, MAIN, E, 0)
    unpack(recv_x, X)
    received(recv_g, MAIN, E, 1)
    unpack(recv_g, G)
    gate_tile = recv_g[:, D + QD : D + QD + 128]
    rest_tile = dot(unpack_pick(0), gate_tile)
    gate_col = jnp.concatenate(
        [
            jnp.broadcast_to(gate_tile[:, 0:1].astype(F32), (S, 128)),
            jnp.broadcast_to(rest_tile[:, 64:65], (R, 128)),
        ],
        axis=0,
    )
    SG[...] = (gate_col[:, 0:1] * G[...].astype(F32)).astype(BF16)
    growr[...] = dot_nt(hot(iota((8, 128), 1) == 0), gate_col.astype(BF16))
    gt[...] = jnp.zeros_like(gt)

    def chunk(c):
        rows = pl.ds(pl.multiple_of(c * FC, FC), FC)
        hidden = dot_nt(w_inT[rows, :], X[...])
        back = dot_nt(w_out[rows, :], G[...])
        square = hidden * hidden
        t = jnp.tanh(gelu_k * (hidden + 0.044715 * (square * hidden)))
        cdf = 0.5 * (1.0 + t)
        active = (hidden * cdf).astype(BF16)
        AT[rows, :] = active
        slope = cdf + hidden * (0.5 * (1.0 - t * t)) * (
            gelu_k * (1.0 + (3.0 * 0.044715) * square)
        )
        HT[rows, :] = ((growr[0:1, :] * back) * slope).astype(BF16)
        gt[0:1, :] += jnp.sum(back * active.astype(F32), axis=0, keepdims=True)

    def at_offset(o):
        return lax.rem(z + o + 2 * NZ, NZ)

    def line_copy(src, buf, s, h, to, k):
        i = s * NSUB + h
        return pltpu.make_async_remote_copy(
            src_ref=src,
            dst_ref=buf.at[pl.ds(pl.multiple_of(i * SUB, SUB), SUB)],
            send_sem=ring_sem.at[2 * k, i],
            recv_sem=ring_sem.at[2 * k + 1, i],
            device_id=(me, to),
            device_id_type=MESH,
        )

    ways = ((AT, SG, cw0, cw, -1), (HT, X, ccw0, ccw, 1))

    def ring_step(s):
        def body(h, c):
            for k, (left, right, buf0, buf, sign) in enumerate(ways):
                src_chunk = at_offset(sign * (1 + s))
                rows = pl.ds(pl.multiple_of(src_chunk * FC + h * SUB, SUB), SUB)
                own = dot(left[rows, :], right[...])
                if s == 0:
                    place_at = buf0.at[pl.ds(pl.multiple_of(h * SUB, SUB), SUB)]
                    place_at[...] = own.astype(BF16)
                else:
                    i = (s - 1) * NSUB + h
                    place_at = buf.at[pl.ds(pl.multiple_of(i * SUB, SUB), SUB)]
                    wait_bytes(place_at, ring_sem.at[2 * k + 1, i])
                    place_at[...] = (own + place_at[...].astype(F32)).astype(BF16)
                line_copy(place_at, buf, s, h, at_offset(-sign), k).start()
            return c

        lax.fori_loop(0, NSUB, body, 0)

    def ring_end():
        outs = (wo, wiT)

        def body(h, c):
            for k, (left, right, buf0, buf, sign) in enumerate(ways):
                rows = pl.ds(pl.multiple_of(z * FC + h * SUB, SUB), SUB)
                own = dot(left[rows, :], right[...])
                i = (NZ - 2) * NSUB + h
                last = buf.at[pl.ds(pl.multiple_of(i * SUB, SUB), SUB)]
                wait_bytes(last, ring_sem.at[2 * k + 1, i])
                here = pl.ds(pl.multiple_of(h * SUB, SUB), SUB)
                outs[k][here, :] = (own + last[...].astype(F32)).astype(BF16)
            return c

        lax.fori_loop(0, NSUB, body, 0)

    computed = set()

    def ensure(offsets):
        for o in offsets:
            if o % NZ not in computed:
                computed.add(o % NZ)
                chunk(at_offset(o))

    def pair(s):
        if 2 * (1 + s) < NZ:
            computed.update({(1 + s) % NZ, (-1 - s) % NZ})

            def body(i, c):
                chunk(at_offset((2 * i - 1) * (1 + s)))
                return c

            lax.fori_loop(0, 2, body, 0)
        else:
            ensure((-1 - s, 1 + s))

    def stats_on():
        received(sr1, 8, E, 2)
        total = sr1[0:8, :]
        for j in range(1, E):
            total += sr1[j * 8 : (j + 1) * 8, :]
        ss2[...] = total
        to_line(ss2, sr2, 8, 3)
        own_block(ss2, False, sr2, z, 8)

    def rows_home():
        ensure(range(NZ))

        def body(i, c):
            rows = pl.ds(pl.multiple_of(i * QD, QD), QD)
            rbT[rows, :] = dot(w_in[rows, :], HT[...]).astype(BF16)
            return c

        lax.fori_loop(0, SPLIT, body, 0)
        eye_s = hot(iota((S, S), 0) == iota((S, S), 1))
        rest = jnp.zeros((S, QD), F32)
        for q in range(SPLIT):
            cols = slice(q * QD, (q + 1) * QD)
            send_b[:, cols] = dot_nt(eye_s, rbT[cols, 0:S]).astype(BF16)
            rest += dot_nt(pack_pick(q), rbT[cols, S:ROWS])
        send_b[:, D : D + QD] = rest.astype(BF16)
        terms = jnp.broadcast_to(gt[0:1, :], (128, ROWS)).astype(BF16)
        r = iota((S, R), 1)
        s_ = iota((S, R), 0)
        any_pick = hot((s_ // MAIN == r // REST) & (lax.rem(s_, REST) == lax.rem(r, REST)))
        term_main = dot_nt(eye_s, terms[:, 0:S])
        term_rest = dot_nt(any_pick, terms[:, S:ROWS])
        send_b[:, D + QD : D + QD + 128] = jnp.where(
            iota((S, 128), 1) < 64, term_main, term_rest
        ).astype(BF16)
        to_plane(send_b, True, recv_b, MAIN, 4)
        own_block(send_b, True, recv_b, me, MAIN)

    def spread_grad(v):
        average = jnp.mean(v, axis=0, keepdims=True)
        dev = jnp.mean((v - average) ** 2, axis=0, keepdims=True)
        return (2.0 * (v - average) - 2.0 * dev / average) / (E * average * average)

    def at_home():
        received(sr2, 8, NZ, 3)
        received(recv_b, MAIN, E, 4)
        total = sr2[0:8, :]
        for j in range(1, NZ):
            total += sr2[j * 8 : (j + 1) * 8, :]
        row = jnp.broadcast_to(total[0:1, :], (E, 128))
        imp = jnp.sum(jnp.where(lane_id == row_id, row, 0.0), axis=1, keepdims=True)
        ld = jnp.sum(jnp.where(lane_id == row_id + E, row, 0.0), axis=1, keepdims=True)
        imp_coef = TOTAL * spread_grad(imp)
        load_coef = TOTAL * spread_grad(ld)
        probs = probs_s[...]
        zscore = z_s[...]
        tile = recv_b[:, D + QD : D + QD + 128].astype(F32)
        weighted = sel[...].astype(F32) * tile[:, 0:1] + selr[0:S, :].astype(F32) * tile[:, 64:65]
        gather = hot(iota((E, S), 1) // MAIN == iota((E, S), 0))
        score = dot(gather, weighted.astype(BF16)) + imp_coef
        noisy_grad = probs * (score - jnp.sum(probs * score, axis=0, keepdims=True))
        z_grad = load_coef * inv_root_tau * jnp.exp(-0.5 * zscore * zscore)
        thresh = thr[...] == iota((E, T), 0)
        logit_grad = (
            noisy_grad
            + z_grad
            - jnp.where(thresh, jnp.sum(z_grad, axis=0, keepdims=True), 0.0)
        )
        low = logit_grad.astype(BF16)
        llT_s[...] = low
        weight_part = dot(low, patches[...])
        bias_col = jnp.sum(logit_grad, axis=1, keepdims=True)
        bias_row = jnp.sum(jnp.where(lane_id == row_id, bias_col, 0.0), axis=0, keepdims=True)
        bias_tile = jnp.broadcast_to(bias_row, (8, 128))
        tiles = D // 128
        for p in range(E):
            a, b = p // tiles, p % tiles
            ws1[p * 16 : p * 16 + 8, :] = weight_part[a * 8 : a * 8 + 8, b * 128 : b * 128 + 128]
            ws1[p * 16 + 8 : p * 16 + 16, :] = bias_tile
        to_plane(ws1, True, wr1, 16, 5)
        own_block(ws1, True, wr1, me, 16)
        low_rows = dot_nt(eye_t, llT_s[...]).astype(BF16)
        for q in range(SPLIT):
            cols = slice(q * QD, (q + 1) * QD)
            out = dot(selT[...], recv_b[:, cols])
            out += dot(selrT[pl.ds(q * T, T), :], recv_b[:, D : D + QD])
            out += dot(low_rows, rwT[:, cols])
            pg[:, cols] = out.astype(BF16)

    def reduce_plane():
        received(wr1, 16, E, 5)
        total = wr1[0:16, :]
        for j in range(1, E):
            total += wr1[j * 16 : (j + 1) * 16, :]
        ws2[...] = total
        to_line(ws2, wr2, 16, 6)
        own_block(ws2, False, wr2, z, 16)

    def reduce_line():
        received(wr2, 16, NZ, 6)
        total = wr2[0:16, :]
        for j in range(1, NZ):
            total += wr2[j * 16 : (j + 1) * 16, :]
        rb[...] = total[8:16, :]
        ws3[...] = total[0:8, :]
        to_plane(ws3, False, wr3, 8, 7)
        own_block(ws3, False, wr3, me, 8)

    def spread_total():
        received(wr3, 8, E, 7)
        tiles = D // 128
        for p in range(E):
            a, b = p // tiles, p % tiles
            rgT[a * 8 : a * 8 + 8, b * 128 : b * 128 + 128] = wr3[p * 8 : p * 8 + 8, :]

    hooks = {}
    late = []
    for k, work in enumerate((rows_home, at_home, reduce_plane, reduce_line, spread_total)):
        at = NZ - 5 + k
        if NZ // 2 - 1 <= NZ - 5 and at < NZ - 1:
            hooks[at] = work
        else:
            late.append(work)
    for s in range(NZ - 1):
        pair(s)
        ring_step(s)
        if s == 0:
            stats_on()
        if s in hooks:
            hooks[s]()
    ensure(range(NZ))
    ring_end()
    for work in late:
        work()

    sent(recv_x, MAIN, E, 0)
    sent(recv_g, MAIN, E, 1)
    sent(sr1, 8, E, 2)
    sent(sr2, 8, NZ, 3)
    sent(recv_b, MAIN, E, 4)
    sent(wr1, 16, E, 5)
    sent(wr2, 16, NZ, 6)
    sent(wr3, 8, E, 7)

    def drain(i, c):
        for k, way in enumerate(ways):
            wait_bytes(way[2].at[pl.ds(0, SUB)], ring_sem.at[2 * k, i])
        return c

    lax.fori_loop(0, (NZ - 1) * NSUB, drain, 0)


def on_device(
    patches, router_weight, router_bias, noise, top_experts, threshold_expert, w_in, w_out, out_grad
):
    T, D = patches.shape
    E = router_weight.shape[1]
    NZ = lax.axis_size("dp")
    F = w_in.shape[2]
    FC = F // NZ
    S = E * MAIN
    ROWS = S + E * REST
    QD = D // SPLIT
    WX = D + QD
    WG = WX + 128
    VMEM = pltpu.VMEM
    whole = pl.BlockSpec(memory_space=pltpu.VMEM)
    far = pl.BlockSpec(memory_space=pl.ANY)
    pg, wiT, wo, rgT, rb = pl.pallas_call(
        functools.partial(kernel, E, NZ, float(T * E * NZ)),
        out_shape=(
            jax.ShapeDtypeStruct((T, D), BF16),
            jax.ShapeDtypeStruct((FC, D), BF16),
            jax.ShapeDtypeStruct((FC, D), BF16),
            jax.ShapeDtypeStruct((E, D), F32),
            jax.ShapeDtypeStruct((8, 128), F32),
        ),
        in_specs=[whole] * 7 + [far] * 2,
        out_specs=(whole,) * 5,
        scratch_shapes=[
            VMEM((D, F), BF16), VMEM((F, D), BF16), VMEM((F, D), BF16),
            VMEM((S, T), BF16), VMEM((SPLIT * S, T), BF16),
            VMEM((T, S), BF16), VMEM((SPLIT * T, S), BF16),
            VMEM((S, WX), BF16), VMEM((S, WG), BF16), VMEM((S, WX), BF16), VMEM((S, WG), BF16),
            VMEM((S, WG), BF16), VMEM((S, WG), BF16),
            VMEM((ROWS, D), BF16), VMEM((ROWS, D), BF16), VMEM((ROWS, D), BF16),
            VMEM((F, ROWS), BF16), VMEM((F, ROWS), BF16), VMEM((D, ROWS), BF16),
            VMEM((8, ROWS), F32), VMEM((8, ROWS), F32),
            VMEM((FC, D), BF16), VMEM(((NZ - 1) * FC, D), BF16),
            VMEM((FC, D), BF16), VMEM(((NZ - 1) * FC, D), BF16),
            VMEM((E, T), F32), VMEM((E, T), F32), VMEM((E, T), BF16),
            VMEM((8, 128), F32), VMEM((E * 8, 128), F32),
            VMEM((8, 128), F32), VMEM((NZ * 8, 128), F32),
            VMEM((E * 16, 128), F32), VMEM((E * 16, 128), F32),
            VMEM((16, 128), F32), VMEM((NZ * 16, 128), F32),
            VMEM((8, 128), F32), VMEM((E * 8, 128), F32),
            pltpu.SemaphoreType.DMA((2,)),
            pltpu.SemaphoreType.DMA((16,)),
            pltpu.SemaphoreType.DMA((4, (NZ - 1) * NSUB)),
        ],
        compiler_params=pltpu.CompilerParams(
            collective_id=0, has_side_effects=True, vmem_limit_bytes=63 * 1024 * 1024
        ),
        name="moe_back",
    )(
        patches,
        router_weight.T,
        router_bias.reshape(E, 1),
        noise.T,
        top_experts.T,
        threshold_expert.reshape(1, T),
        out_grad,
        w_in[0],
        w_out[0],
    )
    return (pg, wiT.T[None], wo[None], rgT.T, rb[0, :E])


def solution(mesh):
    both = ("expert", "dp")
    in_specs = (
        P(both, None), P(), P(), P(both, None), P(both, None), P(both),
        P("expert", None, None), P("expert", None, None), P(both, None),
    )
    out_specs = (P(both, None), P("expert", None, "dp"), P("expert", "dp", None), P(), P())
    return jax.shard_map(
        on_device, mesh=mesh, in_specs=in_specs, out_specs=out_specs, check_vma=False
    )
```

time: 532 us -> 161 us (0.30)
  waiting for transfers between devices: 280 us -> 0 us
  Pallas kernels: 0 us -> 149 us
  blocking collectives: 133 us -> 0 us
  matrix products: 43.4 us -> 0 us
  starting transfers between devices: 22.2 us -> 0 us
  between operations: 19.7 us -> 0.64 us
  other arithmetic: 14.4 us -> 0 us
  local copies, waits for them, and re-layouts: 17.5 us -> 9.87 us
    psum x1 -> x0, waiting for transfers between devices: 224 us -> none  [on_device(): lax.psum((weight_part, jnp.sum(logit_grad, axis=0)), EXPERT_DP)]
    pallas_call x0 -> x1, Pallas kernels: none -> 149 us  [on_device(): pl.pallas_call(functools.partial(kernel, E, NZ, float(T * E * NZ)), out_s...]
    psum x5 -> x0, blocking collectives: 133 us -> none  [the longest x1 76.5 us: on_device(): lax.psum((weight_part, jnp.sum(logit_grad, axis=0)), EXPERT_DP)]
    dot_general x12 -> x0, matrix products: 43.4 us -> none  [the longest x1 9.25 us: expert_local(): jnp.dot(rows_grad, w_second.T, preferred_element_type=jnp.float32)]
    all_to_all x4 -> x0, waiting for transfers between devices: 37.2 us -> none  [the longest x1 19.8 us: on_device(): lax.all_to_all(sent_in, EXPERT, split_axis=0, concat_axis=0, tiled=True)]
    all_to_all x4 -> x0, starting transfers between devices: 21.9 us -> none  [the longest x1 8.58 us: on_device(): lax.all_to_all(sent_gate, EXPERT, split_axis=0, concat_axis=0, tiled=True)]
    reduce_scatter x2 -> x0, waiting for transfers between devices: 19 us -> none  [the longest x1 19 us: on_device(): lax.psum_scatter(second_grad, 'dp', scatter_dimension=0, tiled=True)]
    reshape x6 -> x1, local copies, waits for them, and re-layouts: 7.83 us -> 1.34 us  [on_device(): router_bias.reshape(E, 1)]
  transfers between devices with their start and end apart: 7 -> 0, of which waited for: 5 -> 0; matrix products, arithmetic and copies ran while one was open for 9% -> 0% of each run, Pallas kernels for 0% -> 0%
where the time goes in v1:
time: 161 us; the launch traced here: 160 us
  Pallas kernels  149 us (93%)
  local copies, waits for them, and re-layouts  9.87 us (6%)
    pallas_call x1, Pallas kernels, on_device(): pl.pallas_call(functools.partial(kernel, E, NZ, float(T * E * NZ)), out_s...  149 us
    unnamed x4, local copies, waits for them, and re-layouts  7.34 us

profile of v1, /device:TPU:1, one launch (start us, length us, event | category | flops | bytes accessed | tf_op | source)
XLA Modules:
  0.0 159.6 jit_solution(6313110617847952171)
XLA Ops:
  0.6 1.3 copy.14.bias
  2.0 149.1 %moe_back.1 = (bf16[256,1024]{1,0:T(8,128)(2,1)}, bf16[256,1024]{1,0:T(8,128)(2,1)}, bf16[256,1024]{1,0:T(8,128)(2,1)}, f32[32,1024]{1,0:T(8,128)}, f32[8,128]{1,0:T(8,128)}) custom-call(bf16[256,1024]{1,0:T(8,128)(2,1)} %patches.1, bf16[32,1024]{1,0:T(8,128)(2,1)} %bitcast.19, f32[32,1]{1,0:T(8,128)} %copy.14.bias, f32[32,256]{1,0:T(8,128)} %bitcast.20, ...), custom_call_target="tpu_custom_call" | custom-call | tf_op jit(solution)/shard_map/moe_back/pallas_call | solution.py:491
  151.0 2.0 %copy.15 = bf16[1,1024,256]{2,1,0:T(8,128)(2,1)} copy(bf16[1,1024,256]{1,2,0:T(8,128)(2,1)} %bitcast.17) | data formatting | bytes 1048576
  153.1 1.2 slice_bitcast_fusion
  154.3 1.9 %copy.19 = bf16[256,1024]{1,0:T(8,128)(2,1)} copy(bf16[256,1024]{1,0:T(8,128)(2,1)} %get-tuple-element.25) | data formatting | bytes 1048576
  156.1 1.9 %copy.20 = bf16[1,256,1024]{2,1,0:T(8,128)(2,1)} copy(bf16[1,256,1024]{2,1,0:T(8,128)(2,1)} %bitcast.16) | data formatting | bytes 1048576
  158.0 1.6 copy.21

commit v2 on v1

--- a/solution.py
+++ b/solution.py
@@ -14,7 +14,7 @@
 MAIN = 16
 REST = 4
 SPLIT = 4
-NSUB = 2
+NSUB = 4
 inv_root_two = 0.7071067811865476
 inv_root_tau = 0.3989422804014327
 gelu_k = math.sqrt(2.0 / math.pi)
@@ -42,9 +42,9 @@
 
 def kernel(
     E, NZ, TOTAL,
-    patches, rwT, bias, noiseT, topT, thr, og, w_in_hbm, w_out_hbm,
+    patches_hbm, rwT, bias, noiseT, topT, thr, og_hbm, w_in_hbm, w_out_hbm,
     pg, wiT, wo, rgT, rb,
-    w_in, w_out, w_inT, sel, selr, selT, selrT, send_x, send_g, recv_x, recv_g,
+    patches, og, w_in, w_out, w_inT, picks, slope, own, sel, selr, selT, selrT, send_x, send_g, recv_x, recv_g,
     send_b, recv_b, X, G, SG, AT, HT, rbT, growr, gt, cw0, cw, ccw0, ccw,
     probs_s, z_s, llT_s, stat, sr1, ss2, sr2, ws1, wr1, ws2, wr2, ws3, wr3, wsem, px, ring_sem,
 ):
@@ -59,6 +59,10 @@
     me = lax.axis_index("expert")
     z = lax.axis_index("dp")
 
+    load_patches = pltpu.make_async_copy(patches_hbm, patches, wsem.at[2])
+    load_og = pltpu.make_async_copy(og_hbm, og, wsem.at[3])
+    load_patches.start()
+    load_og.start()
     load_in = pltpu.make_async_copy(w_in_hbm, w_in, wsem.at[0])
     load_out = pltpu.make_async_copy(w_out_hbm, w_out, wsem.at[1])
     load_in.start()
@@ -154,12 +158,15 @@
 
         lax.fori_loop(0, S // RB, body, 0)
 
+    load_patches.wait()
     pack_rows(patches, send_x)
     pl.semaphore_wait(barrier, E + NZ - 2)
     to_plane(send_x, True, recv_x, MAIN, 0)
     own_block(send_x, True, recv_x, me, MAIN)
 
-    logits = dot_nt(rwT[...], patches[...]) + bias[...]
+    bias_pick = iota((E, E), 0) == iota((E, E), 1)
+    bias_rows = jnp.sum(jnp.where(bias_pick, bias[...], 0.0), axis=1, keepdims=True)
+    logits = dot_nt(rwT[...], patches[...]) + bias_rows
     noisy = logits + noiseT[...]
     top = jnp.max(noisy, axis=0, keepdims=True)
     powers = jnp.exp(noisy - top)
@@ -174,6 +181,7 @@
     gate_rest = jnp.sum(jnp.where(is_rest, prob_rows, 0.0), axis=1, keepdims=True)
     low_lanes = iota((S, 128), 1) < 64
     send_g[:, D + QD : D + QD + 128] = jnp.where(low_lanes, gate_main, gate_rest).astype(BF16)
+    load_og.wait()
     pack_rows(og, send_g)
     to_plane(send_g, True, recv_g, MAIN, 1)
     own_block(send_g, True, recv_g, me, MAIN)
@@ -193,6 +201,11 @@
     selT[...] = dot_nt(eye_t, sel[...]).astype(BF16)
     for q in range(SPLIT):
         selrT[pl.ds(q * T, T), :] = dot_nt(eye_t, selr[pl.ds(q * S, S), :]).astype(BF16)
+    for q in range(SPLIT):
+        r = iota((R, S), 0)
+        picks[pl.ds(q * R, R), :] = hot(
+            iota((R, S), 1) == (r // REST) * MAIN + q * REST + lax.rem(r, REST)
+        )
     load_in.wait()
     load_out.wait()
 
@@ -204,8 +217,7 @@
     lax.fori_loop(0, F // 256, turn, 0)
 
     def unpack_pick(q):
-        r = iota((R, S), 0)
-        return hot(iota((R, S), 1) == (r // REST) * MAIN + q * REST + lax.rem(r, REST))
+        return picks[pl.ds(q * R, R), :]
 
     def pack_pick(q):
         r = iota((S, R), 1)
@@ -218,8 +230,21 @@
                 unpack_pick(q), src[:, D : D + QD]
             ).astype(BF16)
 
+    def chunk_a(c, carry):
+        rows = pl.ds(pl.multiple_of(c * FC, FC), FC)
+        hidden = dot_nt(w_inT[rows, :], X[...])
+        square = hidden * hidden
+        t = jnp.tanh(gelu_k * (hidden + 0.044715 * (square * hidden)))
+        cdf = 0.5 * (1.0 + t)
+        AT[rows, :] = (hidden * cdf).astype(BF16)
+        slope[rows, :] = cdf + hidden * (0.5 * (1.0 - t * t)) * (
+            gelu_k * (1.0 + (3.0 * 0.044715) * square)
+        )
+        return carry
+
     received(recv_x, MAIN, E, 0)
     unpack(recv_x, X)
+    lax.fori_loop(0, NZ, chunk_a, 0)
     received(recv_g, MAIN, E, 1)
     unpack(recv_g, G)
     gate_tile = recv_g[:, D + QD : D + QD + 128]
@@ -232,23 +257,12 @@
         axis=0,
     )
     SG[...] = (gate_col[:, 0:1] * G[...].astype(F32)).astype(BF16)
-    growr[...] = dot_nt(hot(iota((8, 128), 1) == 0), gate_col.astype(BF16))
-    gt[...] = jnp.zeros_like(gt)
-
-    def chunk(c):
+
+    def chunk_b(c):
         rows = pl.ds(pl.multiple_of(c * FC, FC), FC)
-        hidden = dot_nt(w_inT[rows, :], X[...])
         back = dot_nt(w_out[rows, :], G[...])
-        square = hidden * hidden
-        t = jnp.tanh(gelu_k * (hidden + 0.044715 * (square * hidden)))
-        cdf = 0.5 * (1.0 + t)
-        active = (hidden * cdf).astype(BF16)
-        AT[rows, :] = active
-        slope = cdf + hidden * (0.5 * (1.0 - t * t)) * (
-            gelu_k * (1.0 + (3.0 * 0.044715) * square)
-        )
-        HT[rows, :] = ((growr[0:1, :] * back) * slope).astype(BF16)
-        gt[0:1, :] += jnp.sum(back * active.astype(F32), axis=0, keepdims=True)
+        HT[rows, :] = ((growr[0:1, :] * back) * slope[rows, :]).astype(BF16)
+        gt[0:1, :] += jnp.sum(back * AT[rows, :].astype(F32), axis=0, keepdims=True)
 
     def at_offset(o):
         return lax.rem(z + o + 2 * NZ, NZ)
@@ -266,20 +280,32 @@
 
     ways = ((AT, SG, cw0, cw, -1), (HT, X, ccw0, ccw, 1))
 
+    def product(s, k):
+        left, right, _, _, sign = ways[k]
+        rows = pl.ds(pl.multiple_of(at_offset(sign * (1 + s)) * FC, FC), FC)
+        own[k * FC : (k + 1) * FC, :] = dot(left[rows, :], right[...])
+
+    def own_piece(k, h):
+        return own[pl.ds(pl.multiple_of(k * FC + h * SUB, SUB), SUB), :]
+
+    def ring_first(k):
+        _, _, buf0, buf, sign = ways[k]
+
+        def body(h, c):
+            place_at = buf0.at[pl.ds(pl.multiple_of(h * SUB, SUB), SUB)]
+            place_at[...] = own_piece(k, h).astype(BF16)
+            line_copy(place_at, buf, 0, h, at_offset(-sign), k).start()
+            return c
+
+        lax.fori_loop(0, NSUB, body, 0)
+
     def ring_step(s):
         def body(h, c):
-            for k, (left, right, buf0, buf, sign) in enumerate(ways):
-                src_chunk = at_offset(sign * (1 + s))
-                rows = pl.ds(pl.multiple_of(src_chunk * FC + h * SUB, SUB), SUB)
-                own = dot(left[rows, :], right[...])
-                if s == 0:
-                    place_at = buf0.at[pl.ds(pl.multiple_of(h * SUB, SUB), SUB)]
-                    place_at[...] = own.astype(BF16)
-                else:
-                    i = (s - 1) * NSUB + h
-                    place_at = buf.at[pl.ds(pl.multiple_of(i * SUB, SUB), SUB)]
-                    wait_bytes(place_at, ring_sem.at[2 * k + 1, i])
-                    place_at[...] = (own + place_at[...].astype(F32)).astype(BF16)
+            for k, (_, _, _, buf, sign) in enumerate(ways):
+                i = (s - 1) * NSUB + h
+                place_at = buf.at[pl.ds(pl.multiple_of(i * SUB, SUB), SUB)]
+                wait_bytes(place_at, ring_sem.at[2 * k + 1, i])
+                place_at[...] = (own_piece(k, h) + place_at[...].astype(F32)).astype(BF16)
                 line_copy(place_at, buf, s, h, at_offset(-sign), k).start()
             return c
 
@@ -289,37 +315,22 @@
         outs = (wo, wiT)
 
         def body(h, c):
-            for k, (left, right, buf0, buf, sign) in enumerate(ways):
-                rows = pl.ds(pl.multiple_of(z * FC + h * SUB, SUB), SUB)
-                own = dot(left[rows, :], right[...])
+            for k, (_, _, _, buf, _) in enumerate(ways):
                 i = (NZ - 2) * NSUB + h
                 last = buf.at[pl.ds(pl.multiple_of(i * SUB, SUB), SUB)]
                 wait_bytes(last, ring_sem.at[2 * k + 1, i])
                 here = pl.ds(pl.multiple_of(h * SUB, SUB), SUB)
-                outs[k][here, :] = (own + last[...].astype(F32)).astype(BF16)
+                outs[k][here, :] = (own_piece(k, h) + last[...].astype(F32)).astype(BF16)
             return c
 
         lax.fori_loop(0, NSUB, body, 0)
 
-    computed = set()
-
-    def ensure(offsets):
-        for o in offsets:
-            if o % NZ not in computed:
-                computed.add(o % NZ)
-                chunk(at_offset(o))
-
-    def pair(s):
-        if 2 * (1 + s) < NZ:
-            computed.update({(1 + s) % NZ, (-1 - s) % NZ})
-
-            def body(i, c):
-                chunk(at_offset((2 * i - 1) * (1 + s)))
-                return c
-
-            lax.fori_loop(0, 2, body, 0)
-        else:
-            ensure((-1 - s, 1 + s))
+    def backs(lo, hi):
+        def body(i, c):
+            chunk_b(at_offset(i))
+            return c
+
+        lax.fori_loop(lo, hi, body, 0)
 
     def stats_on():
         received(sr1, 8, E, 2)
@@ -331,8 +342,6 @@
         own_block(ss2, False, sr2, z, 8)
 
     def rows_home():
-        ensure(range(NZ))
-
         def body(i, c):
             rows = pl.ds(pl.multiple_of(i * QD, QD), QD)
             rbT[rows, :] = dot(w_in[rows, :], HT[...]).astype(BF16)
@@ -435,24 +444,31 @@
             a, b = p // tiles, p % tiles
             rgT[a * 8 : a * 8 + 8, b * 128 : b * 128 + 128] = wr3[p * 8 : p * 8 + 8, :]
 
-    hooks = {}
-    late = []
-    for k, work in enumerate((rows_home, at_home, reduce_plane, reduce_line, spread_total)):
-        at = NZ - 5 + k
-        if NZ // 2 - 1 <= NZ - 5 and at < NZ - 1:
-            hooks[at] = work
-        else:
-            late.append(work)
+    works = (rows_home, at_home, reduce_plane, reduce_line, spread_total)
+    gaps = dict(zip((2, 4, 5, 6), works)) if NZ == 8 else {}
+    product(0, 0)
+    ring_first(0)
+    growr[...] = dot_nt(hot(iota((8, 128), 1) == 0), gate_col.astype(BF16))
+    gt[...] = jnp.zeros_like(gt)
+    backs(1, 2)
+    product(0, 1)
+    ring_first(1)
+    half = NZ // 2
     for s in range(NZ - 1):
-        pair(s)
-        ring_step(s)
+        if s > 0:
+            ring_step(s)
         if s == 0:
+            backs(2, half + 1)
+        if s == 1 or NZ == 2:
+            backs(half + 1, NZ + 1)
+        product(s + 1, 0)
+        product(s + 1, 1)
+        if s == 1 or NZ == 2:
             stats_on()
-        if s in hooks:
-            hooks[s]()
-    ensure(range(NZ))
+        if s in gaps:
+            gaps[s]()
     ring_end()
-    for work in late:
+    for work in works[len(gaps):]:
         work()
 
     sent(recv_x, MAIN, E, 0)
@@ -470,6 +486,14 @@
         return c
 
     lax.fori_loop(0, (NZ - 1) * NSUB, drain, 0)
+
+
+def finish(pg, wiT, wo, rgT, rb, pg_out, wi_out, wo_out, rgT_out, rb_out):
+    pg_out[...] = pg[...]
+    wi_out[...] = wiT[...].T
+    wo_out[...] = wo[...]
+    rgT_out[...] = rgT[...]
+    rb_out[...] = rb[0:1, 0 : rb_out.shape[1]]
 
 
 def on_device(
@@ -497,10 +521,12 @@
             jax.ShapeDtypeStruct((E, D), F32),
             jax.ShapeDtypeStruct((8, 128), F32),
         ),
-        in_specs=[whole] * 7 + [far] * 2,
+        in_specs=[far] + [whole] * 5 + [far] * 3,
         out_specs=(whole,) * 5,
         scratch_shapes=[
+            VMEM((T, D), BF16), VMEM((T, D), BF16),
             VMEM((D, F), BF16), VMEM((F, D), BF16), VMEM((F, D), BF16),
+            VMEM((SPLIT * E * REST, S), BF16), VMEM((F, ROWS), F32), VMEM((2 * FC, D), F32),
             VMEM((S, T), BF16), VMEM((SPLIT * S, T), BF16),
             VMEM((T, S), BF16), VMEM((SPLIT * T, S), BF16),
             VMEM((S, WX), BF16), VMEM((S, WG), BF16), VMEM((S, WX), BF16), VMEM((S, WG), BF16),
@@ -516,7 +542,7 @@
             VMEM((E * 16, 128), F32), VMEM((E * 16, 128), F32),
             VMEM((16, 128), F32), VMEM((NZ * 16, 128), F32),
             VMEM((8, 128), F32), VMEM((E * 8, 128), F32),
-            pltpu.SemaphoreType.DMA((2,)),
+            pltpu.SemaphoreType.DMA((4,)),
             pltpu.SemaphoreType.DMA((16,)),
             pltpu.SemaphoreType.DMA((4, (NZ - 1) * NSUB)),
         ],
@@ -527,7 +553,7 @@
     )(
         patches,
         router_weight.T,
-        router_bias.reshape(E, 1),
+        router_bias.reshape(1, E),
         noise.T,
         top_experts.T,
         threshold_expert.reshape(1, T),
@@ -535,7 +561,20 @@
         w_in[0],
         w_out[0],
     )
-    return (pg, wiT.T[None], wo[None], rgT.T, rb[0, :E])
+    pg, wi, wo, rgT, rb = pl.pallas_call(
+        finish,
+        out_shape=(
+            jax.ShapeDtypeStruct((T, D), BF16),
+            jax.ShapeDtypeStruct((D, FC), BF16),
+            jax.ShapeDtypeStruct((FC, D), BF16),
+            jax.ShapeDtypeStruct((E, D), F32),
+            jax.ShapeDtypeStruct((1, E), F32),
+        ),
+        in_specs=[whole] * 5,
+        out_specs=(whole,) * 5,
+        name="moe_back_out",
+    )(pg, wiT, wo, rgT, rb)
+    return (pg, wi[None], wo[None], rgT.T, rb[0])
 
 
 def solution(mesh):

time: 161 us -> 142 us (0.88)
  local copies, waits for them, and re-layouts: 9.87 us -> 0 us
  Pallas kernels: 149 us -> 140 us
    pallas_call x1, Pallas kernels: 149 us -> 138 us  [on_device(): pl.pallas_call(functools.partial(kernel, E, NZ, float(T * E * NZ)), out_s...]
    unnamed x4 -> x0, local copies, waits for them, and re-layouts: 7.34 us -> none
    pallas_call x0 -> x1, Pallas kernels: none -> 2.72 us  [on_device(): pl.pallas_call(finish, out_shape=(jax.ShapeDtypeStruct((T, D), BF16), jax...]
where the time goes in v2:
time: 142 us; the launch traced here: 141 us
  Pallas kernels  140 us (99%)
    pallas_call x1, Pallas kernels, on_device(): pl.pallas_call(functools.partial(kernel, E, NZ, float(T * E * NZ)), out_s...  138 us

profile of v2, /device:TPU:1, one launch (start us, length us, event | category | flops | bytes accessed | tf_op | source)
XLA Modules:
  0.0 141.1 jit_solution(18291677575976804691)
XLA Ops:
  0.6 137.7 %moe_back.1 = (bf16[256,1024]{1,0:T(8,128)(2,1)}, bf16[256,1024]{1,0:T(8,128)(2,1)}, bf16[256,1024]{1,0:T(8,128)(2,1)}, f32[32,1024]{1,0:T(8,128)}, f32[8,128]{1,0:T(8,128)}) custom-call(bf16[256,1024]{1,0:T(8,128)(2,1)} %patches_hbm.1, bf16[32,1024]{1,0:T(8,128)(2,1)} %bitcast.13, f32[1,32]{1,0:T(1,128)} %bitcast.17, f32[32,256]{1,0:T(8,128)} %bitcast.14, ...), custom_call_target="tpu_custom_call" | custom-call | tf_op jit(solution)/shard_map/moe_back/pallas_call | solution.py:515
  138.3 2.7 %moe_back_out.1 = (bf16[256,1024]{1,0:T(8,128)(2,1)}, bf16[1024,256]{1,0:T(8,128)(2,1)}, bf16[256,1024]{1,0:T(8,128)(2,1)}, f32[32,1024]{1,0:T(8,128)}, f32[1,32]{1,0:T(1,128)}) custom-call(bf16[256,1024]{1,0:T(8,128)(2,1)} %get-tuple-element.15.pg, bf16[256,1024]{1,0:T(8,128)(2,1)} %get-tuple-element.16.wiT, bf16[256,1024]{1,0:T(8,128)(2,1)} %get-tuple-element.17.wo, ...), custom_call_target="tpu_custom_call" | custom-call | tf_op jit(solution)/shard_map/moe_back_out/pallas_call | solution.py:564

commit v3 on v2

--- a/solution.py
+++ b/solution.py
@@ -45,7 +45,7 @@
     patches_hbm, rwT, bias, noiseT, topT, thr, og_hbm, w_in_hbm, w_out_hbm,
     pg, wiT, wo, rgT, rb,
     patches, og, w_in, w_out, w_inT, picks, slope, own, sel, selr, selT, selrT, send_x, send_g, recv_x, recv_g,
-    send_b, recv_b, X, G, SG, AT, HT, rbT, growr, gt, cw0, cw, ccw0, ccw,
+    recv_b, X, G, SG, AT, HT, growr, gt, cw, ccw,
     probs_s, z_s, llT_s, stat, sr1, ss2, sr2, ws1, wr1, ws2, wr2, ws3, wr3, wsem, px, ring_sem,
 ):
     T, D = patches.shape
@@ -84,6 +84,28 @@
 
     lax.fori_loop(1, E, greet_plane, 0)
     lax.fori_loop(1, NZ, greet_line, 0)
+
+    NX = E // 8
+    offsets = [(a, b, c) for a in range(NX) for b in range(4) for c in range(2)][1:]
+    offsets.sort(key=lambda o: -(min(o[0], NX - o[0]) + min(o[1], 4 - o[1])))
+    my_x, my_y, my_c = me // 8, lax.rem(me // 2, 4), lax.rem(me, 2)
+    turn_of = 1 - 2 * my_c
+
+    def to_plane_far(src, dst, rows, k):
+        for a, b, c in offsets:
+            peer = (
+                lax.rem(my_x + turn_of * a + NX, NX) * 8
+                + lax.rem(my_y + turn_of * b + 4, 4) * 2
+                + lax.rem(my_c + c, 2)
+            )
+            pltpu.make_async_remote_copy(
+                src_ref=src.at[pl.ds(pl.multiple_of(peer * rows, rows), rows)],
+                dst_ref=dst.at[pl.ds(pl.multiple_of(me * rows, rows), rows)],
+                send_sem=px.at[2 * k],
+                recv_sem=px.at[2 * k + 1],
+                device_id=(peer, z),
+                device_id_type=MESH,
+            ).start()
 
     def to_plane(src, by_peer, dst, rows, k):
         def body(i, c):
@@ -161,7 +183,7 @@
     load_patches.wait()
     pack_rows(patches, send_x)
     pl.semaphore_wait(barrier, E + NZ - 2)
-    to_plane(send_x, True, recv_x, MAIN, 0)
+    to_plane_far(send_x, recv_x, MAIN, 0)
     own_block(send_x, True, recv_x, me, MAIN)
 
     bias_pick = iota((E, E), 0) == iota((E, E), 1)
@@ -183,7 +205,7 @@
     send_g[:, D + QD : D + QD + 128] = jnp.where(low_lanes, gate_main, gate_rest).astype(BF16)
     load_og.wait()
     pack_rows(og, send_g)
-    to_plane(send_g, True, recv_g, MAIN, 1)
+    to_plane_far(send_g, recv_g, MAIN, 1)
     own_block(send_g, True, recv_g, me, MAIN)
 
     importance = jnp.sum(probs, axis=1, keepdims=True)
@@ -246,17 +268,16 @@
     unpack(recv_x, X)
     lax.fori_loop(0, NZ, chunk_a, 0)
     received(recv_g, MAIN, E, 1)
-    unpack(recv_g, G)
+    for q in range(SPLIT):
+        G[S:ROWS, q * QD : (q + 1) * QD] = dot(
+            unpack_pick(q), recv_g[:, D : D + QD]
+        ).astype(BF16)
     gate_tile = recv_g[:, D + QD : D + QD + 128]
     rest_tile = dot(unpack_pick(0), gate_tile)
-    gate_col = jnp.concatenate(
-        [
-            jnp.broadcast_to(gate_tile[:, 0:1].astype(F32), (S, 128)),
-            jnp.broadcast_to(rest_tile[:, 64:65], (R, 128)),
-        ],
-        axis=0,
-    )
-    SG[...] = (gate_col[:, 0:1] * G[...].astype(F32)).astype(BF16)
+    gate_main = gate_tile[:, 0:1].astype(F32)
+    gate_rest = rest_tile[:, 64:65]
+    SG[0:S, :] = (gate_main * recv_g[:, 0:D].astype(F32)).astype(BF16)
+    SG[S:ROWS, :] = (gate_rest * G[S:ROWS, :].astype(F32)).astype(BF16)
 
     def chunk_b(c):
         rows = pl.ds(pl.multiple_of(c * FC, FC), FC)
@@ -278,6 +299,9 @@
             device_id_type=MESH,
         )
 
+    cw0, ccw0 = w_inT.at[pl.ds(0, FC)], w_inT.at[pl.ds(FC, FC)]
+    rbT = w_inT.at[pl.ds(F // 2, D), 0:ROWS]
+    send_b = send_g
     ways = ((AT, SG, cw0, cw, -1), (HT, X, ccw0, ccw, 1))
 
     def product(s, k):
@@ -348,6 +372,7 @@
             return c
 
         lax.fori_loop(0, SPLIT, body, 0)
+        sent(recv_g, MAIN, E, 1)
         eye_s = hot(iota((S, S), 0) == iota((S, S), 1))
         rest = jnp.zeros((S, QD), F32)
         for q in range(SPLIT):
@@ -364,7 +389,7 @@
         send_b[:, D + QD : D + QD + 128] = jnp.where(
             iota((S, 128), 1) < 64, term_main, term_rest
         ).astype(BF16)
-        to_plane(send_b, True, recv_b, MAIN, 4)
+        to_plane_far(send_b, recv_b, MAIN, 4)
         own_block(send_b, True, recv_b, me, MAIN)
 
     def spread_grad(v):
@@ -448,7 +473,11 @@
     gaps = dict(zip((2, 4, 5, 6), works)) if NZ == 8 else {}
     product(0, 0)
     ring_first(0)
-    growr[...] = dot_nt(hot(iota((8, 128), 1) == 0), gate_col.astype(BF16))
+    G[0:S, :] = recv_g[:, 0:D]
+    first_lane = hot(iota((8, 128), 1) == 0)
+    last_lane = hot(iota((8, 128), 1) == 64)
+    growr[:, 0:S] = dot_nt(first_lane, gate_tile)
+    growr[:, S:ROWS] = dot_nt(last_lane, rest_tile.astype(BF16))
     gt[...] = jnp.zeros_like(gt)
     backs(1, 2)
     product(0, 1)
@@ -472,7 +501,6 @@
         work()
 
     sent(recv_x, MAIN, E, 0)
-    sent(recv_g, MAIN, E, 1)
     sent(sr1, 8, E, 2)
     sent(sr2, 8, NZ, 3)
     sent(recv_b, MAIN, E, 4)
@@ -530,12 +558,12 @@
             VMEM((S, T), BF16), VMEM((SPLIT * S, T), BF16),
             VMEM((T, S), BF16), VMEM((SPLIT * T, S), BF16),
             VMEM((S, WX), BF16), VMEM((S, WG), BF16), VMEM((S, WX), BF16), VMEM((S, WG), BF16),
-            VMEM((S, WG), BF16), VMEM((S, WG), BF16),
+            VMEM((S, WG), BF16),
             VMEM((ROWS, D), BF16), VMEM((ROWS, D), BF16), VMEM((ROWS, D), BF16),
-            VMEM((F, ROWS), BF16), VMEM((F, ROWS), BF16), VMEM((D, ROWS), BF16),
+            VMEM((F, ROWS), BF16), VMEM((F, ROWS), BF16),
             VMEM((8, ROWS), F32), VMEM((8, ROWS), F32),
-            VMEM((FC, D), BF16), VMEM(((NZ - 1) * FC, D), BF16),
-            VMEM((FC, D), BF16), VMEM(((NZ - 1) * FC, D), BF16),
+            VMEM(((NZ - 1) * FC, D), BF16),
+            VMEM(((NZ - 1) * FC, D), BF16),
             VMEM((E, T), F32), VMEM((E, T), F32), VMEM((E, T), BF16),
             VMEM((8, 128), F32), VMEM((E * 8, 128), F32),
             VMEM((8, 128), F32), VMEM((NZ * 8, 128), F32),
@@ -547,7 +575,7 @@
             pltpu.SemaphoreType.DMA((4, (NZ - 1) * NSUB)),
         ],
         compiler_params=pltpu.CompilerParams(
-            collective_id=0, has_side_effects=True, vmem_limit_bytes=63 * 1024 * 1024
+            collective_id=0, has_side_effects=True, vmem_limit_bytes=52 * 1024 * 1024
         ),
         name="moe_back",
     )(
@@ -572,6 +600,7 @@
         ),
         in_specs=[whole] * 5,
         out_specs=(whole,) * 5,
+        compiler_params=pltpu.CompilerParams(vmem_limit_bytes=8 * 1024 * 1024),
         name="moe_back_out",
     )(pg, wiT, wo, rgT, rb)
     return (pg, wi[None], wo[None], rgT.T, rb[0])

time: 142 us -> 134 us (0.944)
  Pallas kernels: 140 us -> 130 us
  local copies, waits for them, and re-layouts: 0 us -> 3.6 us
    pallas_call x1, Pallas kernels: 138 us -> 129 us  [on_device(): pl.pallas_call(functools.partial(kernel, E, NZ, float(T * E * NZ)), out_s...]
    unnamed x0 -> x10, local copies, waits for them, and re-layouts: none -> 3.6 us
where the time goes in v3:
time: 134 us
  Pallas kernels  130 us (97%)
  local copies, waits for them, and re-layouts  3.6 us (3%)
    pallas_call x1, Pallas kernels, on_device(): pl.pallas_call(functools.partial(kernel, E, NZ, float(T * E * NZ)), out_s...  129 us
    unnamed x10, local copies, waits for them, and re-layouts  3.6 us

profile of v3, /device:TPU:1, one launch (start us, length us, event | category | flops | bytes accessed | tf_op | source)
XLA Modules:
  0.0 134.2 jit_solution(16154545763354414745)
XLA Ops:
  0.6 0.0 copy-start
  0.6 0.8 copy-done
  1.5 0.0 copy-start.1
  1.5 0.8 copy-done.1
  2.2 0.0 copy-start.2
  2.2 0.7 copy-done.2
  2.9 0.0 copy-start.3
  2.9 0.7 copy-done.3
  3.6 0.0 copy-start.4
  3.6 0.7 copy-done.4
  4.3 128.6 %moe_back.1 = (bf16[256,1024]{1,0:T(8,128)(2,1)S(1)}, bf16[256,1024]{1,0:T(8,128)(2,1)S(1)}, bf16[256,1024]{1,0:T(8,128)(2,1)S(1)}, f32[32,1024]{1,0:T(8,128)S(1)}, f32[8,128]{1,0:T(8,128)S(1)}) custom-call(bf16[256,1024]{1,0:T(8,128)(2,1)} %patches_hbm.1, bf16[32,1024]{1,0:T(8,128)(2,1)S(1)} %bitcast.11, f32[1,32]{1,0:T(1,128)S(1)} %bitcast.15, ...), custom_call_target="tpu_custom_call" | custom-call | tf_op jit(solution)/shard_map/moe_back/pallas_call | solution.py:543
  132.8 1.3 moe_back_out.1
Async XLA Ops:
  0.6 0.8 copy-start
  1.5 0.8 copy-start.1
  2.2 0.7 copy-start.2
  2.9 0.7 copy-start.3
  3.6 0.7 copy-start.4

commit v4 on v3

--- a/solution.py
+++ b/solution.py
@@ -42,9 +42,9 @@
 
 def kernel(
     E, NZ, TOTAL,
-    patches_hbm, rwT, bias, noiseT, topT, thr, og_hbm, w_in_hbm, w_out_hbm,
-    pg, wiT, wo, rgT, rb,
-    patches, og, w_in, w_out, w_inT, picks, slope, own, sel, selr, selT, selrT, send_x, send_g, recv_x, recv_g,
+    patches_hbm, rwT_hbm, bias_hbm, noiseT_hbm, topT_hbm, thr_hbm, og_hbm, w_in_hbm, w_out_hbm,
+    pg_hbm, wiT_hbm, wo_hbm, rgT_hbm, rb_hbm,
+    pg, wiT, wo, rgT, rb, osem, sgate, rgate, rwT, bias, noiseT, topT, thr, patches, og, w_in, w_out, w_inT, picks, slope, own, sel, selr, selT, selrT, send_x, send_g, recv_x, recv_g,
     recv_b, X, G, SG, AT, HT, growr, gt, cw, ccw,
     probs_s, z_s, llT_s, stat, sr1, ss2, sr2, ws1, wr1, ws2, wr2, ws3, wr3, wsem, px, ring_sem,
 ):
@@ -61,7 +61,16 @@
 
     load_patches = pltpu.make_async_copy(patches_hbm, patches, wsem.at[2])
     load_og = pltpu.make_async_copy(og_hbm, og, wsem.at[3])
+    small = [
+        pltpu.make_async_copy(a, b, wsem.at[4 + i])
+        for i, (a, b) in enumerate(
+            ((topT_hbm, topT), (rwT_hbm, rwT), (bias_hbm, bias), (noiseT_hbm, noiseT), (thr_hbm, thr))
+        )
+    ]
+    small[0].start()
     load_patches.start()
+    for load_small in small[1:]:
+        load_small.start()
     load_og.start()
     load_in = pltpu.make_async_copy(w_in_hbm, w_in, wsem.at[0])
     load_out = pltpu.make_async_copy(w_out_hbm, w_out, wsem.at[1])
@@ -91,7 +100,7 @@
     my_x, my_y, my_c = me // 8, lax.rem(me // 2, 4), lax.rem(me, 2)
     turn_of = 1 - 2 * my_c
 
-    def to_plane_far(src, dst, rows, k):
+    def to_plane_far(src, dst, rows, k, cols):
         for a, b, c in offsets:
             peer = (
                 lax.rem(my_x + turn_of * a + NX, NX) * 8
@@ -99,7 +108,7 @@
                 + lax.rem(my_c + c, 2)
             )
             pltpu.make_async_remote_copy(
-                src_ref=src.at[pl.ds(pl.multiple_of(peer * rows, rows), rows)],
+                src_ref=src.at[pl.ds(pl.multiple_of(peer * rows, rows), rows), 0:cols],
                 dst_ref=dst.at[pl.ds(pl.multiple_of(me * rows, rows), rows)],
                 send_sem=px.at[2 * k],
                 recv_sem=px.at[2 * k + 1],
@@ -153,6 +162,7 @@
         wait_bytes(dst.at[pl.ds(0, (peers - 1) * rows)], px.at[2 * k])
 
     experts = iota((E, T), 0)
+    small[0].wait()
     member = (topT[0:1, :] == experts) | (topT[1:2, :] == experts)
     earlier = hot(iota((T, T), 0) < iota((T, T), 1))
     before = dot(hot(member), earlier)
@@ -183,9 +193,11 @@
     load_patches.wait()
     pack_rows(patches, send_x)
     pl.semaphore_wait(barrier, E + NZ - 2)
-    to_plane_far(send_x, recv_x, MAIN, 0)
+    to_plane_far(send_x, recv_x, MAIN, 0, D + QD)
     own_block(send_x, True, recv_x, me, MAIN)
 
+    for load_small in small[1:]:
+        load_small.wait()
     bias_pick = iota((E, E), 0) == iota((E, E), 1)
     bias_rows = jnp.sum(jnp.where(bias_pick, bias[...], 0.0), axis=1, keepdims=True)
     logits = dot_nt(rwT[...], patches[...]) + bias_rows
@@ -201,12 +213,24 @@
     prob_rows = dot(spread, probs.astype(BF16))
     gate_main = jnp.sum(prob_rows * sel[...].astype(F32), axis=1, keepdims=True)
     gate_rest = jnp.sum(jnp.where(is_rest, prob_rows, 0.0), axis=1, keepdims=True)
-    low_lanes = iota((S, 128), 1) < 64
-    send_g[:, D + QD : D + QD + 128] = jnp.where(low_lanes, gate_main, gate_rest).astype(BF16)
+    lane_s = iota((S, 128), 1)
+    place_s = lax.rem(iota((S, 128), 0), MAIN)
+    gate_at = jnp.where(
+        lane_s == place_s,
+        gate_main,
+        jnp.where((place_s < REST) & (lane_s == MAIN + place_s), gate_rest, 0.0),
+    )
+    by_expert = hot(iota((E, S), 1) // MAIN == iota((E, S), 0))
+    gate_lists = dot(by_expert, gate_at.astype(BF16))
+    for e in range(E):
+        sgate[e] = gate_lists[e : e + 1, :]
+    to_plane(sgate, True, rgate, 1, 8)
+    own_block(sgate, True, rgate, me, 1)
     load_og.wait()
     pack_rows(og, send_g)
-    to_plane_far(send_g, recv_g, MAIN, 1)
-    own_block(send_g, True, recv_g, me, MAIN)
+    to_plane_far(send_g, recv_g, MAIN, 1, D + QD)
+    my_rows = pl.ds(pl.multiple_of(me * MAIN, MAIN), MAIN)
+    recv_g[my_rows, :] = send_g[my_rows, 0 : D + QD]
 
     importance = jnp.sum(probs, axis=1, keepdims=True)
     load = jnp.sum(0.5 * (1.0 + lax.erf(zscore * inv_root_two)), axis=1, keepdims=True)
@@ -267,15 +291,23 @@
     received(recv_x, MAIN, E, 0)
     unpack(recv_x, X)
     lax.fori_loop(0, NZ, chunk_a, 0)
+    received(rgate, 1, E, 8)
+    gate_lists = jnp.concatenate([rgate[e] for e in range(E)], axis=0).astype(BF16)
+    main_lists = dot(hot(iota((S, E), 0) // MAIN == iota((S, E), 1)), gate_lists)
+    rest_lists = dot(hot(iota((R, E), 0) // REST == iota((R, E), 1)), gate_lists)
+    main_here = iota((S, 128), 1) == lax.rem(iota((S, 128), 0), MAIN)
+    rest_here = iota((R, 128), 1) == MAIN + lax.rem(iota((R, 128), 0), REST)
+    gate_main = jnp.sum(jnp.where(main_here, main_lists, 0.0), axis=1, keepdims=True)
+    gate_rest = jnp.sum(jnp.where(rest_here, rest_lists, 0.0), axis=1, keepdims=True)
+    first_lane = hot(iota((8, 128), 1) == 0)
+    growr[:, 0:S] = dot_nt(first_lane, jnp.broadcast_to(gate_main, (S, 128)).astype(BF16))
+    growr[:, S:ROWS] = dot_nt(first_lane, jnp.broadcast_to(gate_rest, (R, 128)).astype(BF16))
+    gt[...] = jnp.zeros_like(gt)
     received(recv_g, MAIN, E, 1)
     for q in range(SPLIT):
         G[S:ROWS, q * QD : (q + 1) * QD] = dot(
             unpack_pick(q), recv_g[:, D : D + QD]
         ).astype(BF16)
-    gate_tile = recv_g[:, D + QD : D + QD + 128]
-    rest_tile = dot(unpack_pick(0), gate_tile)
-    gate_main = gate_tile[:, 0:1].astype(F32)
-    gate_rest = rest_tile[:, 64:65]
     SG[0:S, :] = (gate_main * recv_g[:, 0:D].astype(F32)).astype(BF16)
     SG[S:ROWS, :] = (gate_rest * G[S:ROWS, :].astype(F32)).astype(BF16)
 
@@ -335,6 +367,16 @@
 
         lax.fori_loop(0, NSUB, body, 0)
 
+    whole_outs = [
+        pltpu.make_async_copy(a, b, osem.at[i])
+        for i, (a, b) in enumerate(((pg, pg_hbm), (rb, rb_hbm), (rgT, rgT_hbm)))
+    ]
+
+    def piece_out(k, h):
+        src, dst = ((wo, wo_hbm), (wiT, wiT_hbm))[k]
+        here = pl.ds(pl.multiple_of(h * SUB, SUB), SUB)
+        return pltpu.make_async_copy(src.at[here], dst.at[here], osem.at[3 + k * NSUB + h])
+
     def ring_end():
         outs = (wo, wiT)
 
@@ -345,6 +387,7 @@
                 wait_bytes(last, ring_sem.at[2 * k + 1, i])
                 here = pl.ds(pl.multiple_of(h * SUB, SUB), SUB)
                 outs[k][here, :] = (own_piece(k, h) + last[...].astype(F32)).astype(BF16)
+                piece_out(k, h).start()
             return c
 
         lax.fori_loop(0, NSUB, body, 0)
@@ -389,7 +432,7 @@
         send_b[:, D + QD : D + QD + 128] = jnp.where(
             iota((S, 128), 1) < 64, term_main, term_rest
         ).astype(BF16)
-        to_plane_far(send_b, recv_b, MAIN, 4)
+        to_plane_far(send_b, recv_b, MAIN, 4, D + QD + 128)
         own_block(send_b, True, recv_b, me, MAIN)
 
     def spread_grad(v):
@@ -442,6 +485,7 @@
             out += dot(selrT[pl.ds(q * T, T), :], recv_b[:, D : D + QD])
             out += dot(low_rows, rwT[:, cols])
             pg[:, cols] = out.astype(BF16)
+        whole_outs[0].start()
 
     def reduce_plane():
         received(wr1, 16, E, 5)
@@ -458,6 +502,7 @@
         for j in range(1, NZ):
             total += wr2[j * 16 : (j + 1) * 16, :]
         rb[...] = total[8:16, :]
+        whole_outs[1].start()
         ws3[...] = total[0:8, :]
         to_plane(ws3, False, wr3, 8, 7)
         own_block(ws3, False, wr3, me, 8)
@@ -468,17 +513,13 @@
         for p in range(E):
             a, b = p // tiles, p % tiles
             rgT[a * 8 : a * 8 + 8, b * 128 : b * 128 + 128] = wr3[p * 8 : p * 8 + 8, :]
+        whole_outs[2].start()
 
     works = (rows_home, at_home, reduce_plane, reduce_line, spread_total)
     gaps = dict(zip((2, 4, 5, 6), works)) if NZ == 8 else {}
     product(0, 0)
     ring_first(0)
     G[0:S, :] = recv_g[:, 0:D]
-    first_lane = hot(iota((8, 128), 1) == 0)
-    last_lane = hot(iota((8, 128), 1) == 64)
-    growr[:, 0:S] = dot_nt(first_lane, gate_tile)
-    growr[:, S:ROWS] = dot_nt(last_lane, rest_tile.astype(BF16))
-    gt[...] = jnp.zeros_like(gt)
     backs(1, 2)
     product(0, 1)
     ring_first(1)
@@ -507,6 +548,7 @@
     sent(wr1, 16, E, 5)
     sent(wr2, 16, NZ, 6)
     sent(wr3, 8, E, 7)
+    sent(rgate, 1, E, 8)
 
     def drain(i, c):
         for k, way in enumerate(ways):
@@ -514,6 +556,16 @@
         return c
 
     lax.fori_loop(0, (NZ - 1) * NSUB, drain, 0)
+
+    for copy in whole_outs:
+        copy.wait()
+
+    def written(h, c):
+        piece_out(0, h).wait()
+        piece_out(1, h).wait()
+        return c
+
+    lax.fori_loop(0, NSUB, written, 0)
 
 
 def finish(pg, wiT, wo, rgT, rb, pg_out, wi_out, wo_out, rgT_out, rb_out):
@@ -539,7 +591,7 @@
     WG = WX + 128
     VMEM = pltpu.VMEM
     whole = pl.BlockSpec(memory_space=pltpu.VMEM)
-    far = pl.BlockSpec(memory_space=pl.ANY)
+    far = pl.BlockSpec(memory_space=pltpu.HBM)
     pg, wiT, wo, rgT, rb = pl.pallas_call(
         functools.partial(kernel, E, NZ, float(T * E * NZ)),
         out_shape=(
@@ -549,15 +601,20 @@
             jax.ShapeDtypeStruct((E, D), F32),
             jax.ShapeDtypeStruct((8, 128), F32),
         ),
-        in_specs=[far] + [whole] * 5 + [far] * 3,
-        out_specs=(whole,) * 5,
+        in_specs=[far] * 9,
+        out_specs=(far,) * 5,
         scratch_shapes=[
+            VMEM((T, D), BF16), VMEM((FC, D), BF16), VMEM((FC, D), BF16), VMEM((E, D), F32),
+            VMEM((8, 128), F32), pltpu.SemaphoreType.DMA((3 + 2 * NSUB,)),
+            VMEM((E, 1, 128), F32), VMEM((E, 1, 128), F32),
+            VMEM((E, D), BF16), VMEM((1, E), F32), VMEM((E, T), F32),
+            VMEM((2, T), jnp.int32), VMEM((1, T), jnp.int32),
             VMEM((T, D), BF16), VMEM((T, D), BF16),
             VMEM((D, F), BF16), VMEM((F, D), BF16), VMEM((F, D), BF16),
             VMEM((SPLIT * E * REST, S), BF16), VMEM((F, ROWS), F32), VMEM((2 * FC, D), F32),
             VMEM((S, T), BF16), VMEM((SPLIT * S, T), BF16),
             VMEM((T, S), BF16), VMEM((SPLIT * T, S), BF16),
-            VMEM((S, WX), BF16), VMEM((S, WG), BF16), VMEM((S, WX), BF16), VMEM((S, WG), BF16),
+            VMEM((S, WX), BF16), VMEM((S, WG), BF16), VMEM((S, WX), BF16), VMEM((S, WX), BF16),
             VMEM((S, WG), BF16),
             VMEM((ROWS, D), BF16), VMEM((ROWS, D), BF16), VMEM((ROWS, D), BF16),
             VMEM((F, ROWS), BF16), VMEM((F, ROWS), BF16),
@@ -570,12 +627,12 @@
             VMEM((E * 16, 128), F32), VMEM((E * 16, 128), F32),
             VMEM((16, 128), F32), VMEM((NZ * 16, 128), F32),
             VMEM((8, 128), F32), VMEM((E * 8, 128), F32),
-            pltpu.SemaphoreType.DMA((4,)),
-            pltpu.SemaphoreType.DMA((16,)),
+            pltpu.SemaphoreType.DMA((9,)),
+            pltpu.SemaphoreType.DMA((18,)),
             pltpu.SemaphoreType.DMA((4, (NZ - 1) * NSUB)),
         ],
         compiler_params=pltpu.CompilerParams(
-            collective_id=0, has_side_effects=True, vmem_limit_bytes=52 * 1024 * 1024
+            collective_id=0, has_side_effects=True, vmem_limit_bytes=58 * 1024 * 1024
         ),
         name="moe_back",
     )(
@@ -600,7 +657,7 @@
         ),
         in_specs=[whole] * 5,
         out_specs=(whole,) * 5,
-        compiler_params=pltpu.CompilerParams(vmem_limit_bytes=8 * 1024 * 1024),
+        compiler_params=pltpu.CompilerParams(vmem_limit_bytes=62 * 1024 * 1024),
         name="moe_back_out",
     )(pg, wiT, wo, rgT, rb)
     return (pg, wi[None], wo[None], rgT.T, rb[0])

time: 134 us -> 132 us (0.985)
  local copies, waits for them, and re-layouts: 3.6 us -> 0 us
    unnamed x10 -> x0, local copies, waits for them, and re-layouts: 3.6 us -> none
    pallas_call x1, Pallas kernels: 1.32 us -> 2.72 us  [on_device(): pl.pallas_call(finish, out_shape=(jax.ShapeDtypeStruct((T, D), BF16), jax...]
where the time goes in v4:
time: 132 us
  Pallas kernels  131 us (99%)
    pallas_call x1, Pallas kernels, on_device(): pl.pallas_call(functools.partial(kernel, E, NZ, float(T * E * NZ)), out_s...  128 us
    pallas_call x1, Pallas kernels, on_device(): pl.pallas_call(finish, out_shape=(jax.ShapeDtypeStruct((T, D), BF16), jax...  2.72 us

profile of v4, /device:TPU:1, one launch (start us, length us, event | category | flops | bytes accessed | tf_op | source)
XLA Modules:
  0.0 131.6 jit_solution(11305142737889934511)
XLA Ops:
  0.6 128.2 %moe_back.1 = (bf16[256,1024]{1,0:T(8,128)(2,1)}, bf16[256,1024]{1,0:T(8,128)(2,1)}, bf16[256,1024]{1,0:T(8,128)(2,1)}, f32[32,1024]{1,0:T(8,128)}, f32[8,128]{1,0:T(8,128)}) custom-call(bf16[256,1024]{1,0:T(8,128)(2,1)} %patches_hbm.1, bf16[32,1024]{1,0:T(8,128)(2,1)} %bitcast.13, f32[1,32]{1,0:T(1,128)} %bitcast.17, f32[32,256]{1,0:T(8,128)} %bitcast.14, ...), custom_call_target="tpu_custom_call" | custom-call | tf_op jit(solution)/shard_map/moe_back/pallas_call | solution.py:595
  128.9 2.7 %moe_back_out.1 = (bf16[256,1024]{1,0:T(8,128)(2,1)}, bf16[1024,256]{1,0:T(8,128)(2,1)}, bf16[256,1024]{1,0:T(8,128)(2,1)}, f32[32,1024]{1,0:T(8,128)}, f32[1,32]{1,0:T(1,128)}) custom-call(bf16[256,1024]{1,0:T(8,128)(2,1)} %get-tuple-element.15.pg, bf16[256,1024]{1,0:T(8,128)(2,1)} %get-tuple-element.16.wiT, bf16[256,1024]{1,0:T(8,128)(2,1)} %get-tuple-element.17.wo, ...), custom_call_target="tpu_custom_call" | custom-call | tf_op jit(solution)/shard_map/moe_back_out/pallas_call | solution.py:649

commit v5 on v4

--- a/solution.py
+++ b/solution.py
@@ -14,7 +14,7 @@
 MAIN = 16
 REST = 4
 SPLIT = 4
-NSUB = 4
+NSUB = 2
 inv_root_two = 0.7071067811865476
 inv_root_tau = 0.3989422804014327
 gelu_k = math.sqrt(2.0 / math.pi)
@@ -311,9 +311,14 @@
     SG[0:S, :] = (gate_main * recv_g[:, 0:D].astype(F32)).astype(BF16)
     SG[S:ROWS, :] = (gate_rest * G[S:ROWS, :].astype(F32)).astype(BF16)
 
-    def chunk_b(c):
+    def chunk_b(c, first=False):
         rows = pl.ds(pl.multiple_of(c * FC, FC), FC)
-        back = dot_nt(w_out[rows, :], G[...])
+        if first:
+            back = jnp.concatenate(
+                [dot_nt(w_out[rows, :], recv_g[:, 0:D]), dot_nt(w_out[rows, :], G[S:ROWS, :])], axis=1
+            )
+        else:
+            back = dot_nt(w_out[rows, :], G[...])
         HT[rows, :] = ((growr[0:1, :] * back) * slope[rows, :]).astype(BF16)
         gt[0:1, :] += jnp.sum(back * AT[rows, :].astype(F32), axis=0, keepdims=True)
 
@@ -377,7 +382,7 @@
         here = pl.ds(pl.multiple_of(h * SUB, SUB), SUB)
         return pltpu.make_async_copy(src.at[here], dst.at[here], osem.at[3 + k * NSUB + h])
 
-    def ring_end():
+    def ring_end(lo, hi):
         outs = (wo, wiT)
 
         def body(h, c):
@@ -390,7 +395,7 @@
                 piece_out(k, h).start()
             return c
 
-        lax.fori_loop(0, NSUB, body, 0)
+        lax.fori_loop(lo, hi, body, 0)
 
     def backs(lo, hi):
         def body(i, c):
@@ -478,6 +483,8 @@
             ws1[p * 16 + 8 : p * 16 + 16, :] = bias_tile
         to_plane(ws1, True, wr1, 16, 5)
         own_block(ws1, True, wr1, me, 16)
+
+    def patches_out():
         low_rows = dot_nt(eye_t, llT_s[...]).astype(BF16)
         for q in range(SPLIT):
             cols = slice(q * QD, (q + 1) * QD)
@@ -488,6 +495,7 @@
         whole_outs[0].start()
 
     def reduce_plane():
+        patches_out()
         received(wr1, 16, E, 5)
         total = wr1[0:16, :]
         for j in range(1, E):
@@ -519,10 +527,10 @@
     gaps = dict(zip((2, 4, 5, 6), works)) if NZ == 8 else {}
     product(0, 0)
     ring_first(0)
-    G[0:S, :] = recv_g[:, 0:D]
-    backs(1, 2)
+    chunk_b(at_offset(1), True)
     product(0, 1)
     ring_first(1)
+    G[0:S, :] = recv_g[:, 0:D]
     half = NZ // 2
     for s in range(NZ - 1):
         if s > 0:
@@ -537,9 +545,10 @@
             stats_on()
         if s in gaps:
             gaps[s]()
-    ring_end()
+    ring_end(0, NSUB - 1)
     for work in works[len(gaps):]:
         work()
+    ring_end(NSUB - 1, NSUB)
 
     sent(recv_x, MAIN, E, 0)
     sent(sr1, 8, E, 2)
@@ -568,12 +577,30 @@
     lax.fori_loop(0, NSUB, written, 0)
 
 
-def finish(pg, wiT, wo, rgT, rb, pg_out, wi_out, wo_out, rgT_out, rb_out):
-    pg_out[...] = pg[...]
-    wi_out[...] = wiT[...].T
-    wo_out[...] = wo[...]
-    rgT_out[...] = rgT[...]
-    rb_out[...] = rb[0:1, 0 : rb_out.shape[1]]
+def finish(pg, wiT, wo, rgT, rb, pg_out, wi_out, wo_out, rgT_out, rb_out, a, b, bT, c, d, e, f, sem):
+    def move(src, dst, i):
+        return pltpu.make_async_copy(src, dst, sem.at[i])
+
+    ins = [move(s, t, i) for i, (s, t) in enumerate(((wiT, b), (pg, a), (wo, c), (rgT, d), (rb, e)))]
+    outs = [
+        move(s, t, 5 + i)
+        for i, (s, t) in enumerate(
+            ((bT, wi_out), (a, pg_out), (c, wo_out), (d, rgT_out), (f, rb_out))
+        )
+    ]
+    for copy in ins:
+        copy.start()
+    for i in (1, 2, 3):
+        ins[i].wait()
+        outs[i].start()
+    ins[0].wait()
+    bT[...] = b[...].T
+    outs[0].start()
+    ins[4].wait()
+    f[...] = e[0:1, 0 : f.shape[1]]
+    outs[4].start()
+    for copy in outs:
+        copy.wait()
 
 
 def on_device(
@@ -590,7 +617,6 @@
     WX = D + QD
     WG = WX + 128
     VMEM = pltpu.VMEM
-    whole = pl.BlockSpec(memory_space=pltpu.VMEM)
     far = pl.BlockSpec(memory_space=pltpu.HBM)
     pg, wiT, wo, rgT, rb = pl.pallas_call(
         functools.partial(kernel, E, NZ, float(T * E * NZ)),
@@ -655,8 +681,13 @@
             jax.ShapeDtypeStruct((E, D), F32),
             jax.ShapeDtypeStruct((1, E), F32),
         ),
-        in_specs=[whole] * 5,
-        out_specs=(whole,) * 5,
+        in_specs=[far] * 5,
+        out_specs=(far,) * 5,
+        scratch_shapes=[
+            VMEM((T, D), BF16), VMEM((FC, D), BF16), VMEM((D, FC), BF16), VMEM((FC, D), BF16),
+            VMEM((E, D), F32), VMEM((8, 128), F32), VMEM((1, E), F32),
+            pltpu.SemaphoreType.DMA((10,)),
+        ],
         compiler_params=pltpu.CompilerParams(vmem_limit_bytes=62 * 1024 * 1024),
         name="moe_back_out",
     )(pg, wiT, wo, rgT, rb)

time: 132 us -> 131 us (level)
  no operation moved by 1% of the time
where the time goes in v5:
time: 131 us
  Pallas kernels  130 us (99%)
    pallas_call x1, Pallas kernels, on_device(): pl.pallas_call(functools.partial(kernel, E, NZ, float(T * E * NZ)), out_s...  128 us

profile of v5, /device:TPU:1, one launch (start us, length us, event | category | flops | bytes accessed | tf_op | source)
XLA Modules:
  0.0 131.1 jit_solution(18106182354649023023)
XLA Ops:
  0.6 127.8 %moe_back.1 = (bf16[256,1024]{1,0:T(8,128)(2,1)}, bf16[256,1024]{1,0:T(8,128)(2,1)}, bf16[256,1024]{1,0:T(8,128)(2,1)}, f32[32,1024]{1,0:T(8,128)}, f32[8,128]{1,0:T(8,128)}) custom-call(bf16[256,1024]{1,0:T(8,128)(2,1)} %patches_hbm.1, bf16[32,1024]{1,0:T(8,128)(2,1)} %bitcast.13, f32[1,32]{1,0:T(1,128)} %bitcast.17, f32[32,256]{1,0:T(8,128)} %bitcast.14, ...), custom_call_target="tpu_custom_call" | custom-call | tf_op jit(solution)/shard_map/moe_back/pallas_call | solution.py:621
  128.4 2.5 %moe_back_out.1 = (bf16[256,1024]{1,0:T(8,128)(2,1)}, bf16[1024,256]{1,0:T(8,128)(2,1)}, bf16[256,1024]{1,0:T(8,128)(2,1)}, f32[32,1024]{1,0:T(8,128)}, f32[1,32]{1,0:T(1,128)}) custom-call(bf16[256,1024]{1,0:T(8,128)(2,1)} %get-tuple-element.15.pg, bf16[256,1024]{1,0:T(8,128)(2,1)} %get-tuple-element.16.wiT, bf16[256,1024]{1,0:T(8,128)(2,1)} %get-tuple-element.17.wo, ...), custom_call_target="tpu_custom_call" | custom-call | tf_op jit(solution)/shard_map/moe_back_out/pallas_call | solution.py:675
